TPU v7x, 32 devices: a whole 2x2x4 slice. The times are simulated.
32 devices in a mesh: cell: 16 (over z, y, x), view: 2 (over core).
Axes of the slice: x: 2, y: 2, z: 4, core: 2. Of those that a mesh axis runs over, the one named last changes fastest.
Arguments:
- params: float32 [7, 131072], P(None, 'cell'), may hold values from -4.5 to 4.5
- first_moment: float32 [7, 131072], P(None, 'cell'), may hold values from -6e-05 to 6e-05
- second_moment: float32 [7, 131072], P(None, 'cell'), may hold values from 1e-11 to 1e-08
- camera: float32 [1, 2, 4], P(None, 'view'), may hold values from -0.3 to 0.3
- slot_block: int32 [1, 2, 16, 16, 4], P(None, 'view', 'cell'), may hold values from -1 to 63, as said below
- slot_anchor: float32 [1, 2, 16, 2, 16, 4], P(None, 'view', 'cell'), may hold values from -0.3 to 0.3
- tile_items: int32 [1, 2, 128, 4], P(None, 'view', 'cell'), may hold values from 0 to 63, as said below
- target: float32 [1, 2, 128, 3, 256], P(None, 'view', 'cell'), may hold values from 0 to 1
Outputs:
- new_params: float32 [7, 131072], P(None, 'cell')
- tile_loss: float32 [1, 2, 128], P(None, 'view', 'cell')
Inputs may be any that keep to these rules, and one draw needn't show every extreme that they name: `slot_block`: -1 marks an empty slot; in every step and view each owner receives all 4 slots from some cell. `tile_items`: entry c * 4 + j names the live slot j from cell c to the tile's owner (tile // 8); every live slot is named exactly once, and the 4 entries of a tile come from distinct cells.
All inputs are finite; a program needn't handle non-finite values.
Results may differ from a plain program's by a relative error of at most 0.00035.
Values sent between devices are 32-bit elements; how exact they have to be, the bound alone decides.
No kernel may reach another device: no remote copies, remote signals or barrier semaphores. Data moves between devices by JAX's collectives and lax.ppermute only.
A program may use at most 64 MiB of HBM per device.

v0:
```python
import math

import jax
import jax.numpy as jnp
import numpy as np
from jax import lax
from jax.sharding import PartitionSpec as P

SIDE = 16
BLOCK = 128
TAPS = 11


ssim_weight = 0.2
stable_one = 0.0001
stable_two = 0.0009
learn_rate = 0.1
beta_one = 0.9
beta_two = 0.999
adam_eps = 1e-08
first_step = 1
opacity_cap = 0.1
weight_floor = 0.5
highest = lax.Precision.HIGHEST


def blur_matrix(tile_side, taps_count):
    offsets = np.arange(tile_side)[:, None] - np.arange(tile_side)[None, :]
    kernel = np.exp(-(offsets * offsets) / 4.5) * (np.abs(offsets) <= taps_count // 2)
    kernel = kernel / kernel.sum(axis=1, keepdims=True)
    return jnp.asarray(np.kron(kernel, kernel).T, jnp.float32)


def pixel_grid(tile_side):
    places = jnp.arange(tile_side * tile_side, dtype=jnp.int32)
    grid_x = ((places % tile_side).astype(jnp.float32) + 0.5) / tile_side
    grid_y = ((places // tile_side).astype(jnp.float32) + 0.5) / tile_side
    return (grid_x, grid_y)


def splat_block(block_params, camera_row, anchors, grid_x, grid_y):
    pos_x = block_params[:, 0]
    pos_y = block_params[:, 1]
    mean_u = (1.0 + camera_row[0]) * pos_x + camera_row[1] * pos_y + anchors[:, 0:1]
    mean_w = camera_row[2] * pos_x + (1.0 + camera_row[3]) * pos_y + anchors[:, 1:2]
    inverse = 0.5 * jnp.exp(-2.0 * block_params[:, 2])
    opacity = opacity_cap * jax.nn.sigmoid(block_params[:, 3])
    colours = jax.nn.sigmoid(block_params[:, 4:7])
    delta_x = grid_x[None, None, :] - mean_u[:, :, None]
    delta_y = grid_y[None, None, :] - mean_w[:, :, None]
    alphas = opacity[:, :, None] * jnp.exp(
        -(delta_x * delta_x + delta_y * delta_y) * inverse[:, :, None]
    )
    weighted = jnp.einsum("ncg,ngp->ncp", colours, alphas, precision=highest)
    totals = jnp.sum(alphas, axis=1)
    transmit = jnp.exp(jnp.sum(jnp.log1p(-alphas), axis=1))
    shaded = (1.0 - transmit)[:, None, :] * weighted / jnp.maximum(totals, weight_floor)[:, None, :]
    return jnp.concatenate([shaded, transmit[:, None, :]], axis=1)


def merge_tiles(items):
    fronts = jnp.ones_like(items[:, 0, 3])
    images = jnp.zeros_like(items[:, 0, :3])
    for rank_index in range(items.shape[1]):
        images = images + fronts[:, None, :] * items[:, rank_index, :3]
        fronts = fronts * items[:, rank_index, 3]
    return images


def tile_losses(images, goal_tiles, blur_table):
    tile_count = images.shape[0]
    predicted = images.reshape(tile_count * 3, -1)
    wanted = goal_tiles.reshape(tile_count * 3, -1)
    stacked = jnp.concatenate(
        [predicted, wanted, predicted * predicted, wanted * wanted, predicted * wanted], axis=0
    )
    blurred = jnp.dot(stacked, blur_table, precision=highest, preferred_element_type=jnp.float32)
    local_pred, local_goal, square_pred, square_goal, cross_term = jnp.split(blurred, 5, axis=0)
    var_pred = square_pred - local_pred * local_pred
    var_goal = square_goal - local_goal * local_goal
    cov_both = cross_term - local_pred * local_goal
    similar = (
        (2.0 * local_pred * local_goal + stable_one)
        * (2.0 * cov_both + stable_two)
        / (
            (local_pred * local_pred + local_goal * local_goal + stable_one)
            * (var_pred + var_goal + stable_two)
        )
    )
    residue = predicted - wanted
    values = (1.0 - ssim_weight) * residue * residue + ssim_weight * (1.0 - similar)
    return jnp.mean(values.reshape(tile_count, -1), axis=1)


def in_groups(function, operands, groups):
    shaped = jax.tree.map(
        lambda array: array.reshape((groups, array.shape[0] // groups) + array.shape[1:]), operands
    )
    results = lax.map(lambda pieces: function(*pieces), shaped)
    return jax.tree.map(lambda array: array.reshape((-1,) + array.shape[2:]), results)


def shards(
    params, first_moment, second_moment, camera, slot_block, slot_anchor, tile_items, target
):
    cell_count = lax.axis_size("cell")
    capacity = slot_block.shape[-1]
    tile_dev = tile_items.shape[2]
    depth_count = tile_items.shape[3]
    components = params.shape[0]
    per_cell = params.shape[1]
    block_count = per_cell // BLOCK
    pixels = SIDE * SIDE
    blur_table = blur_matrix(SIDE, TAPS)
    grid_x, grid_y = pixel_grid(SIDE)
    slot_total = cell_count * capacity
    tile_groups = math.gcd(tile_dev, 8)
    current = params
    share_size = per_cell // lax.axis_size("view")
    offset = lax.axis_index("view") * share_size
    moment_one = lax.dynamic_slice_in_dim(first_moment, offset, share_size, 1)
    moment_two = lax.dynamic_slice_in_dim(second_moment, offset, share_size, 1)
    camera_row = camera[0, 0]
    block_ids = slot_block[0, 0, 0].reshape(-1)
    is_live = block_ids >= 0
    safe_ids = jnp.maximum(block_ids, 0)
    anchors = slot_anchor[0, 0, 0].reshape(2, -1).T
    blocks = jnp.transpose(
        jnp.take(current.reshape(components, block_count, BLOCK), safe_ids, axis=1), (1, 0, 2)
    )
    entries = tile_items[0, 0].reshape(-1)
    goal_tiles = target[0, 0]
    arrived = lax.all_to_all(
        blocks.reshape(cell_count, capacity, components, BLOCK),
        "cell",
        split_axis=0,
        concat_axis=0,
        tiled=True,
    )
    arrived_anchors = lax.all_to_all(
        anchors.reshape(cell_count, capacity, 2), "cell", split_axis=0, concat_axis=0, tiled=True
    )
    item_params = jnp.take(arrived.reshape(slot_total, components, BLOCK), entries, axis=0)
    item_anchors = jnp.take(arrived_anchors.reshape(slot_total, 2), entries, axis=0)

    def owner_group(group_params, group_anchors, group_goals):

        def group_loss(inner_params):
            partial_value = splat_block(inner_params, camera_row, group_anchors, grid_x, grid_y)
            return tile_losses(
                merge_tiles(partial_value.reshape(-1, depth_count, 4, pixels)),
                group_goals,
                blur_table,
            )

        group_values, back_fn = jax.vjp(group_loss, group_params)
        return (group_values, back_fn(jnp.ones_like(group_values))[0])

    losses, item_grads = in_groups(
        owner_group, (item_params, item_anchors, goal_tiles), tile_groups
    )
    returned = jnp.zeros((slot_total, components, BLOCK), jnp.float32).at[entries].set(item_grads)
    slot_grads = lax.all_to_all(
        returned.reshape(cell_count, capacity, components, BLOCK),
        "cell",
        split_axis=0,
        concat_axis=0,
        tiled=True,
    ).reshape(slot_total, components, BLOCK)
    loss_rows = [losses]
    selector = ((safe_ids[:, None] == jnp.arange(block_count)[None, :]) & is_live[:, None]).astype(
        jnp.float32
    )
    gradient = jnp.einsum("nb,nck->cbk", selector, slot_grads, precision=highest).reshape(
        components, per_cell
    )
    fix_one = 1.0 - beta_one**first_step
    fix_two = 1.0 - beta_two**first_step
    piece_grad = lax.psum_scatter(gradient, "view", scatter_dimension=1, tiled=True)
    moment_one = beta_one * moment_one + (1.0 - beta_one) * piece_grad
    moment_two = beta_two * moment_two + (1.0 - beta_two) * piece_grad * piece_grad
    owned_part = lax.dynamic_slice_in_dim(current, offset, share_size, 1)
    owned_part = owned_part - learn_rate * (moment_one / fix_one) / (
        jnp.sqrt(moment_two / fix_two) + adam_eps
    )
    current = lax.all_gather(owned_part, "view", axis=1, tiled=True)
    return (current, jnp.stack(loss_rows)[:, None, :])


def solution(mesh):
    placed = (
        P(None, "cell"),
        P(None, "cell"),
        P(None, "cell"),
        P(None, "view", None),
        P(None, "view", "cell", None, None),
        P(None, "view", "cell", None, None, None),
        P(None, "view", "cell", None),
        P(None, "view", "cell", None, None),
    )
    return jax.shard_map(
        shards,
        mesh=mesh,
        in_specs=placed,
        out_specs=(P(None, "cell"), P(None, "view", "cell")),
        check_vma=False,
    )
```

profile of v0, /device:TPU:0, one launch (start us, length us, event | category | flops | bytes accessed | tf_op | source)
XLA Modules:
  0.0 144.4 jit_solution(5597485896693901713)
XLA Ops:
  8.7 8.5 %all-to-all-start.1 = ((f32[16,4,2]{1,2,0:T(2,128)}), f32[16,4,2]{1,2,0:T(2,128)S(1)}, u32[]{:S(2)}, u32[]{:S(2)}) async-start(f32[16,4,2]{1,2,0:T(2,128)} %copy.45), calls=%async_computation.1 | async-start | bytes 32768 | tf_op jit(solution)/shard_map/all_to_all | solution.py:140
  18.3 1.5 %gather_fusion = f32[64,7,128]{2,1,0:T(8,128)S(1)} fusion(f32[7,64,128]{2,0,1:T(8,128)} %bitcast.199, s32[1024]{0:T(1024)S(1)} %pad_clamp_fusion.1), kind=kCustom, calls=%fused_computation | custom fusion | bytes 459008 | tf_op jit(solution)/shard_map/jit(_take)/gather | solution.py:129
  20.8 3.7 %all-to-all-done.1 = f32[16,4,2]{1,2,0:T(2,128)S(1)} async-done(((f32[16,4,2]{1,2,0:T(2,128)}), f32[16,4,2]{1,2,0:T(2,128)S(1)}, u32[]{:S(2)}, u32[]{:S(2)}) %all-to-all-start.1) | async-done | bytes 544 | tf_op jit(solution)/shard_map/all_to_all | solution.py:140
  24.5 3.7 %all-to-all-start = ((f32[16,4,7,128]{3,1,2,0:T(4,128)}), f32[16,4,7,128]{3,1,2,0:T(4,128)S(1)}, u32[]{:S(2)}, u32[]{:S(2)}) async-start(f32[16,4,7,128]{3,1,2,0:T(4,128)} %copy.41), calls=%async_computation | async-start | bytes 458752 | tf_op jit(solution)/shard_map/all_to_all | solution.py:133
  31.1 5.5 %all-to-all-done = f32[16,4,7,128]{3,1,2,0:T(4,128)S(1)} async-done(((f32[16,4,7,128]{3,1,2,0:T(4,128)}), f32[16,4,7,128]{3,1,2,0:T(4,128)S(1)}, u32[]{:S(2)}, u32[]{:S(2)}) %all-to-all-start) | async-done | bytes 229408 | tf_op jit(solution)/shard_map/all_to_all | solution.py:133
  37.5 74.6 %while.17 = (s32[]{:T(128)}, f32[8,1]{0,1:T(1,128)S(1)}, f32[8,4,7,128]{3,2,1,0:T(8,128)S(1)}, f32[8,4,7,128]{3,2,1,0:T(8,128)S(1)}, f32[]{:T(128)}, /*index=5*/...) while((s32[]{:T(128)}, f32[8,1]{0,1:T(1,128)S(1)}, ...), condition=%wide.region_13.14_spmd.clone.clone, body=%wide.region_0.13_spmd.sunk.clone.clone.sunk | while | flops 45164544 | bytes 1323385 | solution.py:99
  38.2 1.3 broadcast_multiply_fusion.7
  43.3 1.4 fusion.136
  44.8 1.3 multiply_add_fusion.11
  47.5 1.3 broadcast_multiply_fusion.7
  52.6 1.4 fusion.136
  54.1 1.3 multiply_add_fusion.11
  56.8 1.3 broadcast_multiply_fusion.7
  61.9 1.4 fusion.136
  63.4 1.3 multiply_add_fusion.11
  66.1 1.3 broadcast_multiply_fusion.7
  71.3 1.4 fusion.136
  72.8 1.3 multiply_add_fusion.11
  75.5 1.3 broadcast_multiply_fusion.7
  80.6 1.4 fusion.136
  82.1 1.3 multiply_add_fusion.11
  84.8 1.3 broadcast_multiply_fusion.7
  89.9 1.4 fusion.136
  94.1 1.3 broadcast_multiply_fusion.7
  99.3 1.4 fusion.136
  103.4 1.3 broadcast_multiply_fusion.7
  108.6 1.4 fusion.136
  112.7 1.5 %scatter_fusion = f32[64,7,128]{2,1,0:T(8,128)S(1)} fusion(f32[64,7,128]{2,1,0:T(8,128)S(1)} %broadcast_in_dim.116, s32[32]{0:T(128)S(1)} %fusion.84, f32[32,7,128]{2,1,0:T(8,128)S(1)} %bitcast.209), kind=kCustom, calls=%fused_computation.3 | custom fusion | bytes 344192 | tf_op jit(solution)/shard_map/scatter | solution.py:162
  114.9 3.5 %all-to-all-start.2 = ((f32[16,4,7,128]{3,1,2,0:T(4,128)}), f32[16,4,7,128]{3,1,2,0:T(4,128)S(1)}, u32[]{:S(2)}, u32[]{:S(2)}) async-start(f32[16,4,7,128]{3,1,2,0:T(4,128)} %copy.51), calls=%async_computation.2 | async-start | bytes 458752 | tf_op jit(solution)/shard_map/all_to_all | solution.py:163
  118.7 8.1 %all-to-all-done.2 = f32[16,4,7,128]{3,1,2,0:T(4,128)S(1)} async-done(((f32[16,4,7,128]{3,1,2,0:T(4,128)}), f32[16,4,7,128]{3,1,2,0:T(4,128)S(1)}, u32[]{:S(2)}, u32[]{:S(2)}) %all-to-all-start.2) | async-done | bytes 229408 | tf_op jit(solution)/shard_map/all_to_all | solution.py:163
  128.0 5.9 %reduce-scatter.2.cloned.1.call-done = f32[7,4096]{1,0:T(8,128)} async-done(((f32[7,8192]{1,0:T(8,128)}), f32[7,4096]{1,0:T(8,128)}) %reduce-scatter.2.cloned.1.call-update) | async-done | bytes 114704 | tf_op jit(solution)/shard_map/reduce_scatter | solution.py:179
  134.8 2.0 %all_gather.3 = f32[7,8192]{1,0:T(8,128)S(1)} all-gather(f32[7,4096]{1,0:T(8,128)S(1)} %fusion.78), channel_id=1, replica_groups=mesh['cell'=16,'view'=2] {'view'}, dimensions={1}, use_global_device_ids=true | all-gather | bytes 344064 | tf_op jit(solution)/shard_map/all_gather | solution.py:186
  (373 shorter events, 50.3 us)
Async XLA Ops:
  8.7 8.5 %copy-start.7 = (s32[1,1,1,16,4]{3,4,2,1,0:T(4,128)S(1)}, s32[1,1,1,16,4]{3,4,2,1,0:T(4,128)}, u32[]{:S(2)}) copy-start(s32[1,1,1,16,4]{3,4,2,1,0:T(4,128)} %param.15) | copy-start | bytes 772
  8.7 15.8 %all-to-all-start.1 = ((f32[16,4,2]{1,2,0:T(2,128)}), f32[16,4,2]{1,2,0:T(2,128)S(1)}, u32[]{:S(2)}, u32[]{:S(2)}) async-start(f32[16,4,2]{1,2,0:T(2,128)} %copy.45), calls=%async_computation.1 | async-start | bytes 32768 | tf_op jit(solution)/shard_map/all_to_all | solution.py:140
  17.4 0.7 copy-start.6
  20.8 7.4 %copy-start.2 = (f32[1,1,4]{2,1,0:T(1,128)S(1)}, f32[1,1,4]{2,1,0:T(1,128)}, u32[]{:S(2)}) copy-start(f32[1,1,4]{2,1,0:T(1,128)} %param.14) | copy-start | bytes 52
  24.5 5.5 %copy-start.5 = (f32[1,1,8,3,256]{4,2,3,1,0:T(8,128)S(1)}, f32[1,1,8,3,256]{4,2,3,1,0:T(8,128)}, u32[]{:S(2)}) copy-start(f32[1,1,8,3,256]{4,2,3,1,0:T(8,128)} %param.18) | copy-start | bytes 73732
  24.5 12.0 %all-to-all-start = ((f32[16,4,7,128]{3,1,2,0:T(4,128)}), f32[16,4,7,128]{3,1,2,0:T(4,128)S(1)}, u32[]{:S(2)}, u32[]{:S(2)}) async-start(f32[16,4,7,128]{3,1,2,0:T(4,128)} %copy.41), calls=%async_computation | async-start | bytes 458752 | tf_op jit(solution)/shard_map/all_to_all | solution.py:133
  36.6 1.0 copy-start
  112.1 0.5 copy-start.8
  114.9 11.9 %all-to-all-start.2 = ((f32[16,4,7,128]{3,1,2,0:T(4,128)}), f32[16,4,7,128]{3,1,2,0:T(4,128)S(1)}, u32[]{:S(2)}, u32[]{:S(2)}) async-start(f32[16,4,7,128]{3,1,2,0:T(4,128)} %copy.51), calls=%async_computation.2 | async-start | bytes 458752 | tf_op jit(solution)/shard_map/all_to_all | solution.py:163
  118.4 15.4 %reduce-scatter.2.cloned.1.call-start = ((), (), s32[]{:S(2)}) async-start(), calls=%async_computation.4 | async-start | bytes 393216 | tf_op jit(solution)/shard_map/reduce_scatter | solution.py:179
  126.8 7.0 %copy-start.4 = (f32[7,8192]{1,0:T(8,128)S(1)}, f32[7,8192]{1,0:T(8,128)}, u32[]{:S(2)}) copy-start(f32[7,8192]{1,0:T(8,128)} %param.12) | copy-start | bytes 688132
  127.1 6.8 %copy-start.3 = (f32[7,8192]{1,0:T(8,128)S(1)}, f32[7,8192]{1,0:T(8,128)}, u32[]{:S(2)}) copy-start(f32[7,8192]{1,0:T(8,128)} %param.13) | copy-start | bytes 688132
  127.9 5.9 %copy-start.1 = (f32[7,8192]{1,0:T(8,128)S(1)}, f32[7,8192]{1,0:T(8,128)}, u32[]{:S(2)}) copy-start(f32[7,8192]{1,0:T(8,128)} %param.11) | copy-start | bytes 688132
Sparse Core Ops, SparseCore 0:
  128.1 5.7 reduce-scatter.1
where the time goes:
time: 145 us; the launch traced here: 144 us
  other arithmetic  34.4 us (24%)
  matrix products  26.9 us (19%)
  waiting for transfers between devices  23.1 us (16%)
  local copies, waits for them, and re-layouts  20.2 us (14%)
  starting transfers between devices  15.7 us (11%)
  between operations  15.5 us (11%)
  loops' own time  6.52 us (4%)
  blocking collectives  1.99 us (1%)
    dot_general x24, matrix products, splat_block(): weighted = jnp.einsum('ncg,ngp->ncp', colours, alphas, precision=highest)  22.9 us
    mul x24, other arithmetic, splat_block(): opacity = opacity_cap * jax.nn.sigmoid(block_params[:, 3])  10.5 us
    add_any x8, other arithmetic, splat_block(): (1.0 + camera_row[0]) * pos_x + camera_row[1] * pos_y + anchors[:, 0:1]  10.3 us
    all_to_all x1, starting transfers between devices, shards(): lax.all_to_all(anchors.reshape(cell_count, capacity, 2), 'cell', split_ax...  8.47 us
    all_to_all x1, waiting for transfers between devices, shards(): lax.all_to_all(returned.reshape(cell_count, capacity, components, BLOCK),...  8.07 us
    another operation x1, loops' own time, in_groups(): results = lax.map(lambda pieces: function(*pieces), shaped)  6.52 us
    reduce_scatter x1, waiting for transfers between devices, shards(): lax.psum_scatter(gradient, 'view', scatter_dimension=1, tiled=True)  5.87 us
    all_to_all x1, waiting for transfers between devices, shards(): lax.all_to_all(blocks.reshape(cell_count, capacity, components, BLOCK), '...  5.47 us
  transfers between devices with their start and end apart: 4, of which 4 were waited for; matrix products, arithmetic and copies ran while one was open for 3% of the time, Pallas kernels for 0%

commit v1 on v0

v1 whole, which is shorter than its diff:
```python
import functools

import jax
import jax.numpy as jnp
import numpy as np
from jax import lax
from jax.experimental import pallas as pl
from jax.experimental.pallas import tpu as pltpu
from jax.sharding import PartitionSpec as P

SIDE = 16
BLOCK = 128
TAPS = 11
PIX = SIDE * SIDE
ROWS = 8

ssim_weight = 0.2
stable_one = 0.0001
stable_two = 0.0009
learn_rate = 0.1
beta_one = 0.9
beta_two = 0.999
adam_eps = 1e-08
first_step = 1
opacity_cap = 0.1
weight_floor = 0.5
highest = lax.Precision.HIGHEST
f32 = jnp.float32
bf16 = jnp.bfloat16
CHUNK = 16

vmem = pl.BlockSpec(memory_space=pltpu.VMEM)
smem = pl.BlockSpec(memory_space=pltpu.SMEM)
anyspace = pl.BlockSpec(memory_space=pl.ANY)


def blur_kron():
    offsets = np.arange(SIDE)[:, None] - np.arange(SIDE)[None, :]
    kernel = np.exp(-(offsets * offsets) / 4.5) * (np.abs(offsets) <= TAPS // 2)
    kernel = kernel / kernel.sum(axis=1, keepdims=True)
    return np.kron(kernel, kernel).astype(np.float32)


def moment_basis():
    places = np.arange(PIX)
    x = (places % SIDE) - (SIDE - 1) / 2
    y = (places // SIDE) - (SIDE - 1) / 2
    rows = np.zeros((ROWS, PIX), np.float32)
    rows[0], rows[1], rows[2], rows[3], rows[4] = 1.0, x, y, x * x, y * y
    return rows


def pack_kernel(block_ref, anchor_ref, camera_ref, params_ref, out_ref):
    capacity, owners = block_ref.shape
    components = params_ref.shape[0]
    xx = 1.0 + camera_ref[0, 0]
    xy = camera_ref[0, 1]
    yx = camera_ref[0, 2]
    yy = 1.0 + camera_ref[0, 3]
    for owner in range(owners):
        for slot in range(capacity):
            block = jnp.maximum(block_ref[slot, owner], 0)
            lanes = pl.ds(pl.multiple_of(block * BLOCK, BLOCK), BLOCK)
            tile = params_ref[:, lanes]
            pos_x, pos_y = tile[0:1], tile[1:2]
            row = owner * capacity + slot
            out_ref[row, 0:1, :] = xx * pos_x + xy * pos_y + anchor_ref[0, slot, owner]
            out_ref[row, 1:2, :] = yx * pos_x + yy * pos_y + anchor_ref[1, slot, owner]
            out_ref[row, 2:components, :] = tile[2:]
            out_ref[row, components:, :] = jnp.zeros((ROWS - components, BLOCK), f32)


def split_pair(value):
    high = value.astype(bf16)
    return high, (value - high.astype(f32)).astype(bf16)


def owner_kernel(
    items_ref, camera_ref, arrived_ref, goal_ref, table_ref, basis_ref,
    back_ref, loss_ref,
    quant_ref, bcast_ref, alpha_ref, split_ref, part_ref, diff_ref, mix_ref, lhs_ref, rhs_ref,
):
    depth, tiles = items_ref.shape
    channels = goal_ref.shape[0]
    count = depth * tiles
    back_ref[...] = jnp.zeros_like(back_ref)
    lane = lax.broadcasted_iota(jnp.int32, (CHUNK, BLOCK), 1)
    grid_x = ((lane % SIDE).astype(f32) + 0.5) / SIDE
    grid_y = [((lane // SIDE + half * (BLOCK // SIDE)).astype(f32) + 0.5) / SIDE for half in range(2)]
    row8 = lax.broadcasted_iota(jnp.int32, (ROWS, BLOCK), 0)

    def quantities(index, carry):
        slot = items_ref[index // tiles, index % tiles]
        raw = arrived_ref[slot]
        sig = jax.nn.sigmoid(raw)
        spread = 0.5 * jnp.exp(-2.0 * raw)
        value = jnp.where(row8 < 2, raw, jnp.where(row8 == 2, spread, jnp.where(row8 == 3, opacity_cap * sig, sig)))
        quant_ref[index] = value
        columns = value.T
        for q in range(4):
            bcast_ref[q, index] = jnp.broadcast_to(columns[:, q : q + 1], (BLOCK, BLOCK))
        return carry

    lax.fori_loop(0, count, quantities, 0, unroll=4)

    def forward(index, carry):
        prods = [None, None]
        for chunk in range(BLOCK // CHUNK):
            part = pl.ds(chunk * CHUNK, CHUNK)
            mean_u, mean_w = bcast_ref[0, index, part, :], bcast_ref[1, index, part, :]
            inverse, opacity = bcast_ref[2, index, part, :], bcast_ref[3, index, part, :]
            delta_x = grid_x - mean_u
            square_x = delta_x * delta_x
            for half in range(2):
                delta_y = grid_y[half] - mean_w
                alpha = opacity * jnp.exp(-(square_x + delta_y * delta_y) * inverse)
                pixels = pl.ds(half * BLOCK, BLOCK)
                alpha_ref[index, part, pixels] = alpha
                high, low = split_pair(alpha)
                split_ref[index, part, pixels] = high
                split_ref[index, pl.ds(BLOCK + chunk * CHUNK, CHUNK), pixels] = low
                clear = 1.0 - alpha
                prods[half] = clear if prods[half] is None else prods[half] * clear
        clears = []
        for half in range(2):
            prod = prods[half][:ROWS] * prods[half][ROWS:]
            for shift in (4, 2, 1):
                prod = prod * pltpu.roll(prod, shift, 0)
            clears.append(prod[0:1])
        value = quant_ref[index]
        colour = jnp.where((row8 >= 4) & (row8 < 7), value, jnp.where(row8 == 7, 1.0, 0.0))
        high, low = split_pair(colour)
        low = jnp.where(row8 == 7, 0.0, low.astype(f32)).astype(bf16)
        left = jnp.concatenate([high, low], axis=0)
        right = jnp.concatenate([high, jnp.zeros_like(low)], axis=0)
        left = jnp.concatenate([left, right], axis=1)
        sums = jnp.dot(left, split_ref[index], preferred_element_type=f32)
        part_ref[index] = sums[:ROWS] + sums[ROWS:]
        for half in range(2):
            part_ref[index, 0:1, pl.ds(half * BLOCK, BLOCK)] = clears[half]
        return carry

    lax.fori_loop(0, count, forward, 0, unroll=2)

    def gathered(row, rank):
        return part_ref[rank * tiles : (rank + 1) * tiles, row, :]

    transmits = [gathered(0, rank) for rank in range(depth)]
    totals = [gathered(7, rank) for rank in range(depth)]
    floors = [jnp.maximum(total, weight_floor) for total in totals]
    ratios = [(1.0 - transmit) / floor for transmit, floor in zip(transmits, floors)]
    weighted = [[gathered(4 + ch, rank) for ch in range(channels)] for rank in range(depth)]
    shaded = [[ratios[rank] * weighted[rank][ch] for ch in range(channels)] for rank in range(depth)]
    fronts = [jnp.ones_like(transmits[0])]
    for rank in range(depth):
        fronts.append(fronts[rank] * transmits[rank])
    images = [sum(fronts[rank] * shaded[rank][ch] for rank in range(depth)) for ch in range(channels)]
    goals = [goal_ref[ch] for ch in range(channels)]
    image = jnp.concatenate(images, axis=0)
    goal = jnp.concatenate(goals, axis=0)
    stacked = jnp.concatenate([image, goal, image * image, goal * goal, image * goal], axis=0)
    blurred = lax.dot_general(stacked, table_ref[...], (((1,), (1,)), ((), ())), precision=highest, preferred_element_type=f32)
    size = channels * tiles
    local_a, local_b, square_a, square_b, cross = [blurred[i * size : (i + 1) * size] for i in range(5)]
    var_a = square_a - local_a * local_a
    var_b = square_b - local_b * local_b
    both = cross - local_a * local_b
    top_one = 2.0 * local_a * local_b + stable_one
    top_two = 2.0 * both + stable_two
    low_one = local_a * local_a + local_b * local_b + stable_one
    low_two = var_a + var_b + stable_two
    under = 1.0 / (low_one * low_two)
    similar = top_one * top_two * under
    residue = image - goal
    values = (1.0 - ssim_weight) * residue * residue + ssim_weight * (1.0 - similar)
    per_tile = values[:tiles]
    for ch in range(1, channels):
        per_tile = per_tile + values[ch * tiles : (ch + 1) * tiles]
    norm = 1.0 / (channels * PIX)
    column = jnp.sum(per_tile, axis=1, keepdims=True) * norm
    loss_ref[...] = jnp.broadcast_to(column, (tiles, BLOCK)).T[0:1, :]
    scale = -ssim_weight * norm
    by_top_one = scale * top_two * under
    by_top_two = scale * top_one * under
    by_low_one = -scale * similar / low_one
    by_low_two = -scale * similar / low_two
    by_local = 2.0 * (local_b * (by_top_one - by_top_two) + local_a * (by_low_one - by_low_two))
    spread = jnp.dot(
        jnp.concatenate([by_local, by_low_two, 2.0 * by_top_two], axis=0),
        table_ref[...], precision=highest, preferred_element_type=f32,
    )
    by_image = (
        (2.0 * (1.0 - ssim_weight) * norm) * residue
        + spread[:size] + 2.0 * image * spread[size : 2 * size] + goal * spread[2 * size :]
    )
    by_image = [by_image[ch * tiles : (ch + 1) * tiles] for ch in range(channels)]
    diff_ref[...] = jnp.zeros_like(diff_ref)

    def spread_rows(row, rank, value):
        diff_ref[rank * tiles : (rank + 1) * tiles, row, :] = value

    by_front = None
    for rank in reversed(range(depth)):
        by_shaded = [fronts[rank] * by_image[ch] for ch in range(channels)]
        by_transmit = -sum(by_shaded[ch] * weighted[rank][ch] for ch in range(channels)) / floors[rank]
        if by_front is not None:
            by_transmit = by_transmit + by_front * fronts[rank]
        own = sum(by_image[ch] * shaded[rank][ch] for ch in range(channels))
        by_front = own if by_front is None else own + by_front * transmits[rank]
        by_floor = -sum(by_shaded[ch] * shaded[rank][ch] for ch in range(channels)) / floors[rank]
        total = totals[rank]
        by_total = by_floor * jnp.where(total > weight_floor, 1.0, jnp.where(total == weight_floor, 0.5, 0.0))
        for q in range(4):
            value = by_shaded[q] * ratios[rank] if q < channels else by_total
            high = value.astype(bf16).astype(f32)
            spread_rows(q, rank, high)
            spread_rows(4 + q, rank, value - high)
            if q < channels:
                spread_rows(8 + q, rank, high)
        spread_rows(11, rank, by_transmit * transmits[rank])

    rhs_ref[...] = jnp.zeros_like(rhs_ref)
    xx = 1.0 + camera_ref[0, 0]
    xy = camera_ref[0, 1]
    yx = camera_ref[0, 2]
    yy = 1.0 + camera_ref[0, 3]
    for block in range(2):
        rhs_ref[0:ROWS, pl.ds(block * PIX, PIX)] = basis_ref[...]

    def backward(index, carry):
        slot = items_ref[index // tiles, index % tiles]
        value = quant_ref[index]
        rows = diff_ref[index]
        by_log = rows[11:12]
        rows = rows.astype(bf16)
        colour = jnp.where((row8 >= 4) & (row8 < 7), value, jnp.where(row8 == 7, 1.0, 0.0))
        high = colour.astype(bf16).astype(f32)
        low = colour - high
        left = jnp.concatenate([high[4:8], high[4:8], low[4:8], jnp.zeros((4, BLOCK), f32)], axis=0)
        mix_ref[...] = jnp.dot(left.T.astype(bf16), rows, preferred_element_type=f32)
        for chunk in range(BLOCK // CHUNK):
            part = pl.ds(chunk * CHUNK, CHUNK)
            for half in range(2):
                pixels = pl.ds(half * BLOCK, BLOCK)
                alpha = alpha_ref[index, part, pixels]
                clear = 1.0 - alpha
                inverse = 1.0 / clear
                grad = alpha * (mix_ref[part, pixels] - by_log[:, half * BLOCK : (half + 1) * BLOCK] * inverse)
                high, low = split_pair(grad)
                lhs_ref[part, pixels] = high
                lhs_ref[part, pl.ds(PIX + half * BLOCK, BLOCK)] = low
        for block in range(2):
            lhs_ref[:, pl.ds((2 + block) * PIX, PIX)] = split_ref[index, pl.ds(block * BLOCK, BLOCK), :]
            rhs_ref[ROWS:, pl.ds((2 + block) * PIX, PIX)] = rows[0:ROWS]
        moments = lax.dot_general(lhs_ref[...], rhs_ref[...], (((1,), (1,)), ((), ())), preferred_element_type=f32).T
        inverse = value[2:3]
        base_x = 0.5 - value[0:1]
        base_y = 0.5 - value[1:2]
        zero, one_x, one_y = moments[0:1], moments[1:2] * (1.0 / SIDE), moments[2:3] * (1.0 / SIDE)
        two = (moments[3:4] + moments[4:5]) * (1.0 / (SIDE * SIDE))
        sum_x = one_x + base_x * zero
        sum_y = one_y + base_y * zero
        sum_r = two + 2.0 * (base_x * one_x + base_y * one_y) + (base_x * base_x + base_y * base_y) * zero
        by_u = 2.0 * inverse * sum_x
        by_w = 2.0 * inverse * sum_y
        back_ref[slot, 0:1, :] = xx * by_u + yx * by_w
        back_ref[slot, 1:2, :] = xy * by_u + yy * by_w
        back_ref[slot, 2:3, :] = 2.0 * inverse * sum_r
        back_ref[slot, 3:4, :] = zero * (1.0 - value[3:4] * (1.0 / opacity_cap))
        shade = value[4:7]
        back_ref[slot, 4:7, :] = (moments[8:11] + moments[12:15]) * shade * (1.0 - shade)
        return carry

    lax.fori_loop(0, count, backward, 0)


def scatter_kernel(block_ref, grads_ref, out_ref):
    capacity, owners = block_ref.shape
    out_ref[...] = jnp.zeros_like(out_ref)
    for owner in range(owners):
        for slot in range(capacity):
            block = block_ref[slot, owner]
            value = jnp.where(block >= 0, grads_ref[owner * capacity + slot], 0.0)
            out_ref[jnp.maximum(block, 0)] += value


def adam_kernel(own_ref, other_ref, params_ref, one_ref, two_ref, out_ref):
    fix_one = 1.0 - beta_one**first_step
    fix_two = 1.0 - beta_two**first_step
    components = params_ref.shape[0]
    for block in range(params_ref.shape[1] // BLOCK):
        lanes = pl.ds(block * BLOCK, BLOCK)
        grad = own_ref[block, 0:components, :]
        if other_ref is not None:
            grad = grad + other_ref[block, 0:components, :]
        one = beta_one * one_ref[:, lanes] + (1.0 - beta_one) * grad
        two = beta_two * two_ref[:, lanes] + (1.0 - beta_two) * grad * grad
        out_ref[:, lanes] = params_ref[:, lanes] - learn_rate * (one / fix_one) / (
            jnp.sqrt(two / fix_two) + adam_eps
        )


def limit(size):
    return pltpu.CompilerParams(vmem_limit_bytes=size * 1024 * 1024)


def shards(params, first_moment, second_moment, camera, slot_block, slot_anchor, tile_items, target):
    cells = lax.axis_size("cell")
    views = lax.axis_size("view")
    capacity = slot_block.shape[-1]
    tiles, depth = tile_items.shape[2:]
    channels = target.shape[3]
    per_cell = params.shape[1]
    blocks = per_cell // BLOCK
    slots = cells * capacity
    count = tiles * depth

    camera_row = camera.reshape(1, 4)
    block_ids = jnp.swapaxes(slot_block, 3, 4).reshape(capacity, cells)
    anchors = jnp.swapaxes(slot_anchor, 4, 5).reshape(2, capacity, cells)
    items = jnp.swapaxes(tile_items, 2, 3).reshape(depth, tiles)
    goals = jnp.transpose(target, (0, 1, 3, 2, 4)).reshape(channels, tiles, PIX)
    slab = jax.ShapeDtypeStruct((slots, ROWS, BLOCK), f32)

    def exchange(array):
        array = array.reshape(cells, capacity, ROWS, BLOCK)
        array = lax.all_to_all(array, "cell", split_axis=0, concat_axis=0, tiled=True)
        return array.reshape(slots, ROWS, BLOCK)

    packed = pl.pallas_call(
        pack_kernel,
        out_shape=slab,
        in_specs=[smem, smem, smem, vmem],
        out_specs=vmem,
        compiler_params=limit(4),
        name="pack",
    )(block_ids, anchors, camera_row, params)
    arrived = exchange(packed)
    back, losses = pl.pallas_call(
        owner_kernel,
        out_shape=(slab, jax.ShapeDtypeStruct((1, tiles), f32)),
        in_specs=[smem, smem, vmem, vmem, vmem, vmem],
        out_specs=(vmem, vmem),
        scratch_shapes=[
            pltpu.VMEM((count, ROWS, BLOCK), f32),
            pltpu.VMEM((4, count, BLOCK, BLOCK), f32),
            pltpu.VMEM((count, BLOCK, PIX), f32),
            pltpu.VMEM((count, 2 * BLOCK, PIX), bf16),
            pltpu.VMEM((count, ROWS, PIX), f32),
            pltpu.VMEM((count, 2 * ROWS, PIX), f32),
            pltpu.VMEM((BLOCK, PIX), f32),
            pltpu.VMEM((BLOCK, 4 * PIX), bf16),
            pltpu.VMEM((2 * ROWS, 4 * PIX), bf16),
        ],
        compiler_params=limit(40),
        name="owner",
    )(items, camera_row, arrived, goals, jnp.asarray(blur_kron()), jnp.asarray(moment_basis(), bf16))
    returned = exchange(back)
    summed = pl.pallas_call(
        scatter_kernel,
        out_shape=jax.ShapeDtypeStruct((blocks, ROWS, BLOCK), f32),
        in_specs=[smem, vmem],
        out_specs=vmem,
        compiler_params=limit(4),
        name="scatter",
    )(block_ids, returned)
    operands = [summed]
    body = adam_kernel
    if views == 2:
        operands.append(lax.ppermute(summed, "view", [(0, 1), (1, 0)]))
    else:
        operands = [lax.psum(summed, "view")]
        body = lambda own, *rest: adam_kernel(own, None, *rest)
    current = pl.pallas_call(
        body,
        out_shape=jax.ShapeDtypeStruct(params.shape, f32),
        in_specs=[vmem] * (len(operands) + 3),
        out_specs=vmem,
        compiler_params=limit(4),
        name="adam",
    )(*operands, params, first_moment, second_moment)
    return current, losses.reshape(1, 1, tiles)


def solution(mesh):
    placed = (
        P(None, "cell"),
        P(None, "cell"),
        P(None, "cell"),
        P(None, "view", None),
        P(None, "view", "cell", None, None),
        P(None, "view", "cell", None, None, None),
        P(None, "view", "cell", None),
        P(None, "view", "cell", None, None),
    )
    return jax.shard_map(
        shards,
        mesh=mesh,
        in_specs=placed,
        out_specs=(P(None, "cell"), P(None, "view", "cell")),
        check_vma=False,
    )
```

time: 145 us -> 65.5 us (0.45)
  other arithmetic: 34.4 us -> 0 us
  Pallas kernels: 0 us -> 29 us
  blocking collectives: 1.99 us -> 30.9 us
  matrix products: 26.9 us -> 0 us
  waiting for transfers between devices: 23.1 us -> 1.52 us
  local copies, waits for them, and re-layouts: 20.2 us -> 3.01 us
  starting transfers between devices: 15.7 us -> 0.07 us
  between operations: 15.5 us -> 0.7 us
  loops' own time: 6.52 us -> 0 us
    all_to_all x0 -> x2, blocking collectives: none -> 30.9 us  [exchange(): lax.all_to_all(array, 'cell', split_axis=0, concat_axis=0, tiled=True)]
    pallas_call x0 -> x4, Pallas kernels: none -> 29 us  [the longest x1 26.4 us: shards(): pl.pallas_call(owner_kernel, out_shape=(slab, jax.ShapeDtypeStruct((1, ti...]
    dot_general x41 -> x0, matrix products: 26.9 us -> none  [the longest x24 22.9 us: splat_block(): weighted = jnp.einsum('ncg,ngp->ncp', colours, alphas, precision=highest)]
    all_to_all x3 -> x0, waiting for transfers between devices: 17.3 us -> none  [the longest x1 8.07 us: shards(): lax.all_to_all(returned.reshape(cell_count, capacity, components, BLOCK),...]
    all_to_all x3 -> x0, starting transfers between devices: 15.7 us -> none  [the longest x1 8.47 us: shards(): lax.all_to_all(anchors.reshape(cell_count, capacity, 2), 'cell', split_ax...]
    add_any x24 -> x0, other arithmetic: 15.6 us -> none  [the longest x8 10.3 us: splat_block(): (1.0 + camera_row[0]) * pos_x + camera_row[1] * pos_y + anchors[:, 0:1]]
    mul x104 -> x0, other arithmetic: 11.4 us -> none  [the longest x24 10.5 us: splat_block(): opacity = opacity_cap * jax.nn.sigmoid(block_params[:, 3])]
    another operation x1 -> x0, loops' own time: 6.52 us -> none  [in_groups(): results = lax.map(lambda pieces: function(*pieces), shaped)]
  transfers between devices with their start and end apart: 4 -> 1, of which waited for: 4 -> 1; matrix products, arithmetic and copies ran while one was open for 3% -> 0% of each run, Pallas kernels for 0% -> 0%
where the time goes in v1:
time: 65.5 us; the launch traced here: 65.2 us
  blocking collectives  30.9 us (47%)
  Pallas kernels  29 us (44%)
  local copies, waits for them, and re-layouts  3.01 us (5%)
  waiting for transfers between devices  1.52 us (2%)
  between operations  0.7 us (1%)
    all_to_all x2, blocking collectives, exchange(): lax.all_to_all(array, 'cell', split_axis=0, concat_axis=0, tiled=True)  30.9 us
    pallas_call x1, Pallas kernels, shards(): pl.pallas_call(owner_kernel, out_shape=(slab, jax.ShapeDtypeStruct((1, ti...  26.4 us
    unnamed x22, local copies, waits for them, and re-layouts  3.01 us
    ppermute x1, waiting for transfers between devices, shards(): operands.append(lax.ppermute(summed, 'view', [(0, 1), (1, 0)]))  1.52 us
  transfers between devices with their start and end apart: 1, of which 1 were waited for; matrix products, arithmetic and copies ran while one was open for 0% of the time, Pallas kernels for 0%

profile of v1, /device:TPU:0, one launch (start us, length us, event | category | flops | bytes accessed | tf_op | source)
XLA Modules:
  0.0 65.2 jit_solution(7543415213792816916)
XLA Ops:
  0.6 0.0 copy-start.6
  0.6 0.0 copy-start.10
  0.7 0.7 %copy-done.6 = s32[1,1,1,16,4]{3,4,2,1,0:T(4,128)S(1)} copy-done((s32[1,1,1,16,4]{3,4,2,1,0:T(4,128)S(1)}, s32[1,1,1,16,4]{3,4,2,1,0:T(4,128)}, u32[]{:S(2)}) %copy-start.6) | copy-done | bytes 280
  1.3 0.0 copy-done.10
  1.3 0.0 copy-start
  1.3 0.9 %copy-done = f32[7,8192]{1,0:T(8,128)S(1)} copy-done((f32[7,8192]{1,0:T(8,128)S(1)}, f32[7,8192]{1,0:T(8,128)}, u32[]{:S(2)}) %copy-start) | copy-done | bytes 229400
  2.3 0.0 copy-start.7
  2.3 0.7 %copy-done.7 = f32[1,1,1,2,16,4]{4,5,3,2,1,0:T(4,128)S(1)} copy-done((f32[1,1,1,2,16,4]{4,5,3,2,1,0:T(4,128)S(1)}, f32[1,1,1,2,16,4]{4,5,3,2,1,0:T(4,128)}, u32[]{:S(2)}) %copy-start.7) | copy-done | bytes 536
  3.0 0.8 %pack.1 = f32[64,8,128]{2,1,0:T(8,128)S(1)} custom-call(s32[4,16]{1,0:T(4,128)S(1)} %bitcast.23, f32[2,4,16]{2,1,0:T(4,128)S(1)} %bitcast.25, f32[1,4]{1,0:T(1,128)S(1)} %bitcast.27, f32[7,8192]{1,0:T(8,128)S(1)} %copy-done), custom_call_target="tpu_custom_call" | custom-call | tf_op jit(solution)/shard_map/pack/pallas_call | solution.py:330
  3.8 0.0 copy-start.2
  3.8 0.0 copy-start.5
  3.8 0.0 copy-start.9
  3.8 18.1 %all_to_all.10 = f32[16,4,8,128]{3,2,1,0:T(8,128)S(1)} all-to-all(f32[16,4,8,128]{3,2,1,0:T(8,128)S(1)} %bitcast.19), channel_id=1, replica_groups=mesh['cell'=16,'view'=2] {'cell'}, dimensions={0} | all-to-all | bytes 524288 | tf_op jit(solution)/shard_map/all_to_all | solution.py:327
  21.9 0.0 copy-start.8
  21.9 0.0 copy-done.2
  21.9 0.0 copy-done.5
  21.9 0.0 copy-done.9
  22.0 0.7 %copy-done.8 = bf16[8,256]{1,0:T(8,128)(2,1)S(1)} copy-done((bf16[8,256]{1,0:T(8,128)(2,1)S(1)}, bf16[8,256]{1,0:T(8,128)(2,1)}, u32[]{:S(2)}) %copy-start.8) | copy-done | bytes 4120
  22.6 26.4 %owner.1 = (f32[64,8,128]{2,1,0:T(8,128)S(1)}, f32[1,8]{1,0:T(1,128)}) custom-call(s32[4,8]{1,0:T(4,128)S(1)} %bitcast.26, f32[1,4]{1,0:T(1,128)S(1)} %bitcast.28, f32[64,8,128]{2,1,0:T(8,128)S(1)} %bitcast.18, f32[3,8,256]{2,1,0:T(8,128)S(1)} %bitcast.22, f32[256,256]{1,0:T(8,128)S(1)} %copy-done.2, bf16[8,256]{1,0:T(8,128)(2,1)S(1)} %copy-done.8), custom_call_target="tpu_custom_call" | custom-call | tf_op jit(solution)/shard_map/owner/pallas_call | solution.py:339
  49.0 0.0 copy-start.4
  49.0 12.7 %all_to_all.11 = f32[16,4,8,128]{3,2,1,0:T(8,128)S(1)} all-to-all(f32[16,4,8,128]{3,2,1,0:T(8,128)S(1)} %bitcast.21), channel_id=1, replica_groups=mesh['cell'=16,'view'=2] {'cell'}, dimensions={0} | all-to-all | bytes 524288 | tf_op jit(solution)/shard_map/all_to_all | solution.py:327
  61.8 0.0 copy-start.1
  61.8 0.0 copy-start.3
  61.8 0.9 %scatter.1.own_ref = f32[64,8,128]{2,1,0:T(8,128)S(1)} custom-call(s32[4,16]{1,0:T(4,128)S(1)} %bitcast.24, f32[64,8,128]{2,1,0:T(8,128)S(1)} %bitcast.20), custom_call_target="tpu_custom_call" | custom-call | tf_op jit(solution)/shard_map/scatter/pallas_call | solution.py:359
  62.6 0.1 collective-permute-start
  62.7 1.5 %collective-permute-done.other_ref = f32[64,8,128]{2,1,0:T(8,128)S(1)} collective-permute-done((f32[64,8,128]{2,1,0:T(8,128)S(1)}, f32[64,8,128]{2,1,0:T(8,128)S(1)}, u32[]{:S(2)}, u32[]{:S(2)}) %collective-permute-start) | collective-permute-done | bytes 262176 | tf_op jit(solution)/shard_map/ppermute | solution.py:370
  64.2 0.0 copy-done.4
  64.2 0.0 copy-done.1
  64.2 0.0 copy-done.3
  64.3 0.9 %adam.1 = f32[7,8192]{1,0:T(8,128)} custom-call(f32[64,8,128]{2,1,0:T(8,128)S(1)} %scatter.1.own_ref, f32[64,8,128]{2,1,0:T(8,128)S(1)} %collective-permute-done.other_ref, f32[7,8192]{1,0:T(8,128)S(1)} %copy-done.1, f32[7,8192]{1,0:T(8,128)S(1)} %copy-done.3, f32[7,8192]{1,0:T(8,128)S(1)} %copy-done.4), custom_call_target="tpu_custom_call" | custom-call | tf_op jit(solution)/shard_map/adam/pallas_call | solution.py:374
Async XLA Ops:
  0.6 0.7 %copy-start.6 = (s32[1,1,1,16,4]{3,4,2,1,0:T(4,128)S(1)}, s32[1,1,1,16,4]{3,4,2,1,0:T(4,128)}, u32[]{:S(2)}) copy-start(s32[1,1,1,16,4]{3,4,2,1,0:T(4,128)} %param.14) | copy-start | bytes 772
  0.6 0.7 %copy-start.10 = (f32[1,1,4]{2,1,0:T(1,128)S(1)}, f32[1,1,4]{2,1,0:T(1,128)}, u32[]{:S(2)}) copy-start(f32[1,1,4]{2,1,0:T(1,128)} %param.13) | copy-start | bytes 52
  1.3 1.0 %copy-start = (f32[7,8192]{1,0:T(8,128)S(1)}, f32[7,8192]{1,0:T(8,128)}, u32[]{:S(2)}) copy-start(f32[7,8192]{1,0:T(8,128)} %params_ref.3) | copy-start | bytes 688132
  2.3 0.7 %copy-start.7 = (f32[1,1,1,2,16,4]{4,5,3,2,1,0:T(4,128)S(1)}, f32[1,1,1,2,16,4]{4,5,3,2,1,0:T(4,128)}, u32[]{:S(2)}) copy-start(f32[1,1,1,2,16,4]{4,5,3,2,1,0:T(4,128)} %param.15) | copy-start | bytes 1540
  3.8 18.2 %copy-start.2 = (f32[256,256]{1,0:T(8,128)S(1)}, f32[256,256]{1,0:T(8,128)}, u32[]{:S(2)}) copy-start(f32[256,256]{1,0:T(8,128)} %constant.4.clone.table_ref) | copy-start | bytes 786436
  3.8 18.2 %copy-start.5 = (f32[1,1,8,3,256]{4,2,3,1,0:T(8,128)S(1)}, f32[1,1,8,3,256]{4,2,3,1,0:T(8,128)}, u32[]{:S(2)}) copy-start(f32[1,1,8,3,256]{4,2,3,1,0:T(8,128)} %param.17) | copy-start | bytes 73732
  3.8 18.2 %copy-start.9 = (s32[1,1,8,4]{2,3,1,0:T(4,128)S(1)}, s32[1,1,8,4]{2,3,1,0:T(4,128)}, u32[]{:S(2)}) copy-start(s32[1,1,8,4]{2,3,1,0:T(4,128)} %param.16) | copy-start | bytes 388
  21.9 0.7 %copy-start.8 = (bf16[8,256]{1,0:T(8,128)(2,1)S(1)}, bf16[8,256]{1,0:T(8,128)(2,1)}, u32[]{:S(2)}) copy-start(bf16[8,256]{1,0:T(8,128)(2,1)} %constant.5.clone.basis_ref) | copy-start | bytes 12292
  49.0 15.2 %copy-start.4 = (f32[7,8192]{1,0:T(8,128)S(1)}, f32[7,8192]{1,0:T(8,128)}, u32[]{:S(2)}) copy-start(f32[7,8192]{1,0:T(8,128)} %two_ref.1) | copy-start | bytes 688132
  61.8 2.5 %copy-start.1 = (f32[7,8192]{1,0:T(8,128)S(1)}, f32[7,8192]{1,0:T(8,128)}, u32[]{:S(2)}) copy-start(f32[7,8192]{1,0:T(8,128)} %params_ref.3) | copy-start | bytes 688132
  61.8 2.5 %copy-start.3 = (f32[7,8192]{1,0:T(8,128)S(1)}, f32[7,8192]{1,0:T(8,128)}, u32[]{:S(2)}) copy-start(f32[7,8192]{1,0:T(8,128)} %one_ref.1) | copy-start | bytes 688132
  62.6 1.6 %collective-permute-start = (f32[64,8,128]{2,1,0:T(8,128)S(1)}, f32[64,8,128]{2,1,0:T(8,128)S(1)}, u32[]{:S(2)}, u32[]{:S(2)}) collective-permute-start(f32[64,8,128]{2,1,0:T(8,128)S(1)} %scatter.1.own_ref), channel_id=1, source_target_pairs={{0,1},{1,0},{2,3},{3,2},{4,5},{5,4},{6,7},{7,6},{8,9},{9,8},{10,11... | collective-permute-start | bytes 786440 | tf_op jit(solution)/shard_map/ppermute | solution.py:370

commit v2 on v1

--- a/solution.py
+++ b/solution.py
@@ -28,10 +28,11 @@
 f32 = jnp.float32
 bf16 = jnp.bfloat16
 CHUNK = 16
+UNROLL = (8, 8, 8, 8)
 
 vmem = pl.BlockSpec(memory_space=pltpu.VMEM)
 smem = pl.BlockSpec(memory_space=pltpu.SMEM)
-anyspace = pl.BlockSpec(memory_space=pl.ANY)
+hbm = pl.BlockSpec(memory_space=pltpu.HBM)
 
 
 def blur_kron():
@@ -41,18 +42,22 @@
     return np.kron(kernel, kernel).astype(np.float32)
 
 
-def moment_basis():
-    places = np.arange(PIX)
-    x = (places % SIDE) - (SIDE - 1) / 2
-    y = (places // SIDE) - (SIDE - 1) / 2
-    rows = np.zeros((ROWS, PIX), np.float32)
-    rows[0], rows[1], rows[2], rows[3], rows[4] = 1.0, x, y, x * x, y * y
-    return rows
-
-
-def pack_kernel(block_ref, anchor_ref, camera_ref, params_ref, out_ref):
+def pack_kernel(
+    block_hbm, anchor_hbm, camera_hbm, params_hbm, items_hbm,
+    out_ref, items_ref, row_ref,
+    block_ref, anchor_ref, camera_ref, params_ref, sems,
+):
     capacity, owners = block_ref.shape
     components = params_ref.shape[0]
+    pairs = (
+        (params_hbm, params_ref), (block_hbm, block_ref), (anchor_hbm, anchor_ref), (camera_hbm, camera_ref),
+        (items_hbm, items_ref), (camera_hbm, row_ref),
+    )
+    copies = [pltpu.make_async_copy(source, target, sems.at[i]) for i, (source, target) in enumerate(pairs)]
+    for copy in copies:
+        copy.start()
+    for copy in copies:
+        copy.wait()
     xx = 1.0 + camera_ref[0, 0]
     xy = camera_ref[0, 1]
     yx = camera_ref[0, 2]
@@ -76,18 +81,17 @@
 
 
 def owner_kernel(
-    items_ref, camera_ref, arrived_ref, goal_ref, table_ref, basis_ref,
+    items_ref, camera_ref, arrived_ref, goal_ref, table_ref,
     back_ref, loss_ref,
-    quant_ref, bcast_ref, alpha_ref, split_ref, part_ref, diff_ref, mix_ref, lhs_ref, rhs_ref,
+    quant_ref, left_ref, factor_ref, turned_ref, alpha_ref, split_ref, part_ref, diff_ref, lhs_ref,
 ):
     depth, tiles = items_ref.shape
     channels = goal_ref.shape[0]
     count = depth * tiles
+    halves = PIX // BLOCK
     back_ref[...] = jnp.zeros_like(back_ref)
-    lane = lax.broadcasted_iota(jnp.int32, (CHUNK, BLOCK), 1)
-    grid_x = ((lane % SIDE).astype(f32) + 0.5) / SIDE
-    grid_y = [((lane // SIDE + half * (BLOCK // SIDE)).astype(f32) + 0.5) / SIDE for half in range(2)]
     row8 = lax.broadcasted_iota(jnp.int32, (ROWS, BLOCK), 0)
+    places = (lax.broadcasted_iota(jnp.int32, (SIDE, BLOCK), 0).astype(f32) + 0.5) / SIDE
 
     def quantities(index, carry):
         slot = items_ref[index // tiles, index % tiles]
@@ -96,60 +100,64 @@
         spread = 0.5 * jnp.exp(-2.0 * raw)
         value = jnp.where(row8 < 2, raw, jnp.where(row8 == 2, spread, jnp.where(row8 == 3, opacity_cap * sig, sig)))
         quant_ref[index] = value
-        columns = value.T
-        for q in range(4):
-            bcast_ref[q, index] = jnp.broadcast_to(columns[:, q : q + 1], (BLOCK, BLOCK))
+        delta_x = places - value[0:1]
+        delta_y = places - value[1:2]
+        factor_x = jnp.exp(-(delta_x * delta_x) * value[2:3])
+        factor_y = value[3:4] * jnp.exp(-(delta_y * delta_y) * value[2:3])
+        factor_ref[index, 0:SIDE, :] = factor_x
+        factor_ref[index, SIDE:, :] = factor_y
+        colour = jnp.where(row8 == 7, 1.0, jnp.where(row8 >= 4, value, 0.0))
+        high = colour.astype(bf16).astype(f32)
+        low = colour - high
+        left = jnp.concatenate([pltpu.roll(low, 5, 0), high + pltpu.roll(high, 4, 0)], axis=0)
+        left_ref[index] = left.astype(bf16)
+        turned_ref[index] = left.T.astype(bf16)
         return carry
 
-    lax.fori_loop(0, count, quantities, 0, unroll=4)
+    lax.fori_loop(0, count, quantities, 0, unroll=UNROLL[0])
 
     def forward(index, carry):
-        prods = [None, None]
-        for chunk in range(BLOCK // CHUNK):
-            part = pl.ds(chunk * CHUNK, CHUNK)
-            mean_u, mean_w = bcast_ref[0, index, part, :], bcast_ref[1, index, part, :]
-            inverse, opacity = bcast_ref[2, index, part, :], bcast_ref[3, index, part, :]
-            delta_x = grid_x - mean_u
-            square_x = delta_x * delta_x
-            for half in range(2):
-                delta_y = grid_y[half] - mean_w
-                alpha = opacity * jnp.exp(-(square_x + delta_y * delta_y) * inverse)
-                pixels = pl.ds(half * BLOCK, BLOCK)
-                alpha_ref[index, part, pixels] = alpha
+        factor_x = jnp.concatenate([factor_ref[index, 0:SIDE, :]] * (BLOCK // SIDE), axis=0).T
+        factor_y = factor_ref[index, SIDE:, :]
+        prods = [None] * halves
+        for half in range(halves):
+            tall = [
+                jnp.broadcast_to(factor_y[half * ROWS + row : half * ROWS + row + 1], (SIDE, BLOCK)) for row in range(ROWS)
+            ]
+            tall = jnp.concatenate(tall, axis=0).T
+            for chunk in range(BLOCK // CHUNK):
+                rows = slice(chunk * CHUNK, (chunk + 1) * CHUNK)
+                alpha = factor_x[rows] * tall[rows]
+                alpha_ref[index, half, rows, :] = alpha
                 high, low = split_pair(alpha)
-                split_ref[index, part, pixels] = high
-                split_ref[index, pl.ds(BLOCK + chunk * CHUNK, CHUNK), pixels] = low
+                split_ref[index, half, rows, :] = high
+                split_ref[index, half, pl.ds(BLOCK + chunk * CHUNK, CHUNK), :] = low
                 clear = 1.0 - alpha
                 prods[half] = clear if prods[half] is None else prods[half] * clear
-        clears = []
-        for half in range(2):
+        left = left_ref[index]
+        right = jnp.concatenate([split_ref[index, half] for half in range(halves)], axis=1)
+        sums = jnp.dot(jnp.concatenate([left, left], axis=1), right, preferred_element_type=f32)
+        sums = sums[ROWS:] + pltpu.roll(sums[:ROWS], ROWS - 1, 0)
+        for half in range(halves):
             prod = prods[half][:ROWS] * prods[half][ROWS:]
             for shift in (4, 2, 1):
                 prod = prod * pltpu.roll(prod, shift, 0)
-            clears.append(prod[0:1])
-        value = quant_ref[index]
-        colour = jnp.where((row8 >= 4) & (row8 < 7), value, jnp.where(row8 == 7, 1.0, 0.0))
-        high, low = split_pair(colour)
-        low = jnp.where(row8 == 7, 0.0, low.astype(f32)).astype(bf16)
-        left = jnp.concatenate([high, low], axis=0)
-        right = jnp.concatenate([high, jnp.zeros_like(low)], axis=0)
-        left = jnp.concatenate([left, right], axis=1)
-        sums = jnp.dot(left, split_ref[index], preferred_element_type=f32)
-        part_ref[index] = sums[:ROWS] + sums[ROWS:]
-        for half in range(2):
-            part_ref[index, 0:1, pl.ds(half * BLOCK, BLOCK)] = clears[half]
+            part_ref[half, pl.ds(pl.multiple_of(index * ROWS, ROWS), ROWS), :] = jnp.where(
+                row8 == 4, prod, sums[:, half * BLOCK : (half + 1) * BLOCK]
+            )
         return carry
 
-    lax.fori_loop(0, count, forward, 0, unroll=2)
+    lax.fori_loop(0, count, forward, 0, unroll=UNROLL[1])
 
     def gathered(row, rank):
-        return part_ref[rank * tiles : (rank + 1) * tiles, row, :]
-
-    transmits = [gathered(0, rank) for rank in range(depth)]
-    totals = [gathered(7, rank) for rank in range(depth)]
+        rows = pl.ds(rank * tiles * ROWS + row, tiles, stride=ROWS)
+        return jnp.concatenate([part_ref[half, rows, :] for half in range(halves)], axis=1)
+
+    transmits = [gathered(4, rank) for rank in range(depth)]
+    totals = [gathered(3, rank) for rank in range(depth)]
     floors = [jnp.maximum(total, weight_floor) for total in totals]
     ratios = [(1.0 - transmit) / floor for transmit, floor in zip(transmits, floors)]
-    weighted = [[gathered(4 + ch, rank) for ch in range(channels)] for rank in range(depth)]
+    weighted = [[gathered(ch, rank) for ch in range(channels)] for rank in range(depth)]
     shaded = [[ratios[rank] * weighted[rank][ch] for ch in range(channels)] for rank in range(depth)]
     fronts = [jnp.ones_like(transmits[0])]
     for rank in range(depth):
@@ -197,7 +205,9 @@
     diff_ref[...] = jnp.zeros_like(diff_ref)
 
     def spread_rows(row, rank, value):
-        diff_ref[rank * tiles : (rank + 1) * tiles, row, :] = value
+        rows = pl.ds(rank * tiles * 2 * ROWS + row, tiles, stride=2 * ROWS)
+        for half in range(halves):
+            diff_ref[half, rows, :] = value[:, half * BLOCK : (half + 1) * BLOCK]
 
     by_front = None
     for rank in reversed(range(depth)):
@@ -213,46 +223,61 @@
         for q in range(4):
             value = by_shaded[q] * ratios[rank] if q < channels else by_total
             high = value.astype(bf16).astype(f32)
-            spread_rows(q, rank, high)
-            spread_rows(4 + q, rank, value - high)
+            spread_rows(8 + q, rank, high)
+            spread_rows(12 + q, rank, value - high)
             if q < channels:
-                spread_rows(8 + q, rank, high)
-        spread_rows(11, rank, by_transmit * transmits[rank])
-
-    rhs_ref[...] = jnp.zeros_like(rhs_ref)
+                spread_rows(1 + q, rank, high)
+        spread_rows(0, rank, by_transmit * transmits[rank])
+
     xx = 1.0 + camera_ref[0, 0]
     xy = camera_ref[0, 1]
     yx = camera_ref[0, 2]
     yy = 1.0 + camera_ref[0, 3]
-    for block in range(2):
-        rhs_ref[0:ROWS, pl.ds(block * PIX, PIX)] = basis_ref[...]
+
+    def item_rows(index):
+        rows = pl.ds(pl.multiple_of(index * 2 * ROWS, 2 * ROWS), 2 * ROWS)
+        return jnp.concatenate([diff_ref[half, rows, :] for half in range(halves)], axis=1)
 
     def backward(index, carry):
+        rows = item_rows(index)
+        by_log = rows[0:1]
+        mix = jnp.dot(turned_ref[index], rows.astype(bf16), preferred_element_type=f32)
+        for half in range(halves):
+            start = half * BLOCK
+            for chunk in range(BLOCK // CHUNK):
+                part = slice(chunk * CHUNK, (chunk + 1) * CHUNK)
+                alpha = alpha_ref[index, half, part, :]
+                inverse = 1.0 / (1.0 - alpha)
+                grad = alpha * (mix[part, start : start + BLOCK] - by_log[:, start : start + BLOCK] * inverse)
+                high, low = split_pair(grad)
+                lhs_ref[index, half, part, :] = high
+                lhs_ref[index, halves + half, part, :] = low
+        return carry
+
+    lax.fori_loop(0, count, backward, 0, unroll=UNROLL[2])
+
+    places = lax.broadcasted_iota(jnp.int32, (2 * ROWS, PIX), 1)
+    row16 = lax.broadcasted_iota(jnp.int32, (2 * ROWS, PIX), 0)
+    middle = (SIDE - 1) / 2
+    cell_x = (places % SIDE).astype(f32) - middle
+    cell_y = (places // SIDE).astype(f32) - middle
+    basis = jnp.where(row16 == 0, 1.0, 0.0)
+    for row, value in enumerate((cell_x, cell_y, cell_x * cell_x, cell_y * cell_y)):
+        basis = jnp.where(row16 == row + 1, value, basis)
+    basis = basis.astype(bf16)
+    basis = jnp.concatenate([basis, basis], axis=1)
+    lower = row16 >= ROWS
+    contract = (((1,), (1,)), ((), ()))
+
+    def finish(index, carry):
         slot = items_ref[index // tiles, index % tiles]
         value = quant_ref[index]
-        rows = diff_ref[index]
-        by_log = rows[11:12]
-        rows = rows.astype(bf16)
-        colour = jnp.where((row8 >= 4) & (row8 < 7), value, jnp.where(row8 == 7, 1.0, 0.0))
-        high = colour.astype(bf16).astype(f32)
-        low = colour - high
-        left = jnp.concatenate([high[4:8], high[4:8], low[4:8], jnp.zeros((4, BLOCK), f32)], axis=0)
-        mix_ref[...] = jnp.dot(left.T.astype(bf16), rows, preferred_element_type=f32)
-        for chunk in range(BLOCK // CHUNK):
-            part = pl.ds(chunk * CHUNK, CHUNK)
-            for half in range(2):
-                pixels = pl.ds(half * BLOCK, BLOCK)
-                alpha = alpha_ref[index, part, pixels]
-                clear = 1.0 - alpha
-                inverse = 1.0 / clear
-                grad = alpha * (mix_ref[part, pixels] - by_log[:, half * BLOCK : (half + 1) * BLOCK] * inverse)
-                high, low = split_pair(grad)
-                lhs_ref[part, pixels] = high
-                lhs_ref[part, pl.ds(PIX + half * BLOCK, BLOCK)] = low
-        for block in range(2):
-            lhs_ref[:, pl.ds((2 + block) * PIX, PIX)] = split_ref[index, pl.ds(block * BLOCK, BLOCK), :]
-            rhs_ref[ROWS:, pl.ds((2 + block) * PIX, PIX)] = rows[0:ROWS]
-        moments = lax.dot_general(lhs_ref[...], rhs_ref[...], (((1,), (1,)), ((), ())), preferred_element_type=f32).T
+        rows = jnp.where(lower, item_rows(index), 0.0).astype(bf16)
+        left = [lhs_ref[index, i] for i in range(2 * halves)] + [split_ref[index, i, 0:BLOCK, :] for i in range(halves)]
+        moments = lax.dot_general(
+            jnp.concatenate(left, axis=1), jnp.concatenate([basis, rows], axis=1), contract, preferred_element_type=f32
+        )
+        moments = moments.T
         inverse = value[2:3]
         base_x = 0.5 - value[0:1]
         base_y = 0.5 - value[1:2]
@@ -271,17 +296,19 @@
         back_ref[slot, 4:7, :] = (moments[8:11] + moments[12:15]) * shade * (1.0 - shade)
         return carry
 
-    lax.fori_loop(0, count, backward, 0)
-
-
-def scatter_kernel(block_ref, grads_ref, out_ref):
+    lax.fori_loop(0, count, finish, 0, unroll=UNROLL[3])
+
+
+def scatter_kernel(block_ref, grads_ref, out_ref, *spare_refs):
     capacity, owners = block_ref.shape
-    out_ref[...] = jnp.zeros_like(out_ref)
-    for owner in range(owners):
-        for slot in range(capacity):
-            block = block_ref[slot, owner]
-            value = jnp.where(block >= 0, grads_ref[owner * capacity + slot], 0.0)
-            out_ref[jnp.maximum(block, 0)] += value
+    sums = (out_ref, *spare_refs)
+    for target in sums:
+        target[...] = jnp.zeros_like(target)
+    for index in range(owners * capacity):
+        block = block_ref[index % capacity, index // capacity]
+        value = jnp.where(block >= 0, grads_ref[index], 0.0)
+        sums[index % len(sums)][jnp.maximum(block, 0)] += value
+    out_ref[...] = sum(target[...] for target in sums)
 
 
 def adam_kernel(own_ref, other_ref, params_ref, one_ref, two_ref, out_ref):
@@ -314,6 +341,7 @@
     blocks = per_cell // BLOCK
     slots = cells * capacity
     count = tiles * depth
+    halves = PIX // BLOCK
 
     camera_row = camera.reshape(1, 4)
     block_ids = jnp.swapaxes(slot_block, 3, 4).reshape(capacity, cells)
@@ -327,40 +355,48 @@
         array = lax.all_to_all(array, "cell", split_axis=0, concat_axis=0, tiled=True)
         return array.reshape(slots, ROWS, BLOCK)
 
-    packed = pl.pallas_call(
+    packed, items, camera_row = pl.pallas_call(
         pack_kernel,
-        out_shape=slab,
-        in_specs=[smem, smem, smem, vmem],
-        out_specs=vmem,
+        out_shape=(slab, jax.ShapeDtypeStruct(items.shape, items.dtype), jax.ShapeDtypeStruct(camera_row.shape, f32)),
+        in_specs=[hbm] * 5,
+        out_specs=(vmem, vmem, vmem),
+        scratch_shapes=[
+            pltpu.SMEM(block_ids.shape, jnp.int32),
+            pltpu.SMEM(anchors.shape, f32),
+            pltpu.SMEM(camera_row.shape, f32),
+            pltpu.VMEM(params.shape, f32),
+            pltpu.SemaphoreType.DMA((6,)),
+        ],
         compiler_params=limit(4),
         name="pack",
-    )(block_ids, anchors, camera_row, params)
+    )(*[pltpu.with_memory_space_constraint(array, pltpu.HBM) for array in (block_ids, anchors, camera_row, params, items)])
     arrived = exchange(packed)
     back, losses = pl.pallas_call(
         owner_kernel,
         out_shape=(slab, jax.ShapeDtypeStruct((1, tiles), f32)),
-        in_specs=[smem, smem, vmem, vmem, vmem, vmem],
+        in_specs=[smem, smem, vmem, vmem, vmem],
         out_specs=(vmem, vmem),
         scratch_shapes=[
             pltpu.VMEM((count, ROWS, BLOCK), f32),
-            pltpu.VMEM((4, count, BLOCK, BLOCK), f32),
-            pltpu.VMEM((count, BLOCK, PIX), f32),
-            pltpu.VMEM((count, 2 * BLOCK, PIX), bf16),
-            pltpu.VMEM((count, ROWS, PIX), f32),
-            pltpu.VMEM((count, 2 * ROWS, PIX), f32),
-            pltpu.VMEM((BLOCK, PIX), f32),
-            pltpu.VMEM((BLOCK, 4 * PIX), bf16),
-            pltpu.VMEM((2 * ROWS, 4 * PIX), bf16),
+            pltpu.VMEM((count, 2 * ROWS, BLOCK), bf16),
+            pltpu.VMEM((count, 2 * SIDE, BLOCK), f32),
+            pltpu.VMEM((count, BLOCK, 2 * ROWS), bf16),
+            pltpu.VMEM((count, halves, BLOCK, BLOCK), f32),
+            pltpu.VMEM((count, halves, 2 * BLOCK, BLOCK), bf16),
+            pltpu.VMEM((halves, count * ROWS, BLOCK), f32),
+            pltpu.VMEM((halves, count * 2 * ROWS, BLOCK), f32),
+            pltpu.VMEM((count, 2 * halves, BLOCK, BLOCK), bf16),
         ],
         compiler_params=limit(40),
         name="owner",
-    )(items, camera_row, arrived, goals, jnp.asarray(blur_kron()), jnp.asarray(moment_basis(), bf16))
+    )(items, camera_row, arrived, goals, jnp.asarray(blur_kron()))
     returned = exchange(back)
     summed = pl.pallas_call(
         scatter_kernel,
         out_shape=jax.ShapeDtypeStruct((blocks, ROWS, BLOCK), f32),
         in_specs=[smem, vmem],
         out_specs=vmem,
+        scratch_shapes=[pltpu.VMEM((blocks, ROWS, BLOCK), f32)] * 3,
         compiler_params=limit(4),
         name="scatter",
     )(block_ids, returned)

time: 65.5 us -> 45.6 us (0.70)
  Pallas kernels: 29 us -> 12.2 us
  local copies, waits for them, and re-layouts: 3.01 us -> 0.03 us
    pallas_call x1, Pallas kernels: 26.4 us -> 9.27 us  [shards(): pl.pallas_call(owner_kernel, out_shape=(slab, jax.ShapeDtypeStruct((1, ti...]
    unnamed x22 -> x12, local copies, waits for them, and re-layouts: 3.01 us -> 0.03 us
where the time goes in v2:
time: 45.6 us; the launch traced here: 45.4 us
  blocking collectives  30.9 us (68%)
  Pallas kernels  12.2 us (27%)
  waiting for transfers between devices  1.52 us (3%)
  between operations  0.68 us (1%)
    all_to_all x2, blocking collectives, exchange(): lax.all_to_all(array, 'cell', split_axis=0, concat_axis=0, tiled=True)  30.9 us
    pallas_call x1, Pallas kernels, shards(): pl.pallas_call(owner_kernel, out_shape=(slab, jax.ShapeDtypeStruct((1, ti...  9.27 us
    ppermute x1, waiting for transfers between devices, shards(): operands.append(lax.ppermute(summed, 'view', [(0, 1), (1, 0)]))  1.52 us
    pallas_call x1, Pallas kernels, shards(): pl.pallas_call(pack_kernel, out_shape=(slab, jax.ShapeDtypeStruct(items.s...  1.2 us
  transfers between devices with their start and end apart: 1, of which 1 were waited for; matrix products, arithmetic and copies ran while one was open for 0% of the time, Pallas kernels for 0%

profile of v2, /device:TPU:0, one launch (start us, length us, event | category | flops | bytes accessed | tf_op | source)
XLA Modules:
  0.0 45.4 jit_solution(11272364319782191565)
XLA Ops:
  0.6 1.2 %pack.1 = (f32[64,8,128]{2,1,0:T(8,128)S(1)}, s32[4,8]{1,0:T(4,128)S(1)}, f32[1,4]{1,0:T(1,128)S(1)}) custom-call(s32[4,16]{1,0:T(4,128)} %bitcast.23, f32[2,4,16]{2,1,0:T(4,128)} %bitcast.25, f32[1,4]{1,0:T(1,128)} %bitcast.27, f32[7,8192]{1,0:T(8,128)} %params_ref.1, s32[4,8]{1,0:T(4,128)} %bitcast.26), custom_call_target="tpu_custom_call" | custom-call | tf_op jit(solution)/shard_map/pack/pallas_call | solution.py:358
  1.8 0.0 copy-start.1
  1.9 0.0 copy-start.4
  1.9 18.1 %all_to_all.10 = f32[16,4,8,128]{3,2,1,0:T(8,128)S(1)} all-to-all(f32[16,4,8,128]{3,2,1,0:T(8,128)S(1)} %bitcast.21), channel_id=1, replica_groups=mesh['cell'=16,'view'=2] {'cell'}, dimensions={0} | all-to-all | bytes 524288 | tf_op jit(solution)/shard_map/all_to_all | solution.py:355
  20.0 0.0 copy-done.1
  20.0 0.0 copy-done.4
  20.0 9.3 %owner.1 = (f32[64,8,128]{2,1,0:T(8,128)S(1)}, f32[1,8]{1,0:T(1,128)}) custom-call(s32[4,8]{1,0:T(4,128)S(1)} %get-tuple-element.7.items_ref, f32[1,4]{1,0:T(1,128)S(1)} %get-tuple-element.8.camera_ref, f32[64,8,128]{2,1,0:T(8,128)S(1)} %bitcast.18, f32[3,8,256]{2,1,0:T(8,128)S(1)} %bitcast.22, f32[256,256]{1,0:T(8,128)S(1)} %copy-done.1), custom_call_target="tpu_custom_call" | custom-call | tf_op jit(solution)/shard_map/owner/pallas_call | solution.py:374
  29.3 0.0 copy-start.5
  29.3 0.0 copy-start.3
  29.3 12.7 %all_to_all.11 = f32[16,4,8,128]{3,2,1,0:T(8,128)S(1)} all-to-all(f32[16,4,8,128]{3,2,1,0:T(8,128)S(1)} %bitcast.20), channel_id=1, replica_groups=mesh['cell'=16,'view'=2] {'cell'}, dimensions={0} | all-to-all | bytes 524288 | tf_op jit(solution)/shard_map/all_to_all | solution.py:355
  42.0 0.0 copy-done.5
  42.0 0.0 copy-start
  42.0 0.0 copy-start.2
  42.0 0.8 %scatter.1.own_ref = f32[64,8,128]{2,1,0:T(8,128)S(1)} custom-call(s32[4,16]{1,0:T(4,128)S(1)} %bitcast.24, f32[64,8,128]{2,1,0:T(8,128)S(1)} %bitcast.19), custom_call_target="tpu_custom_call" | custom-call | tf_op jit(solution)/shard_map/scatter/pallas_call | solution.py:394
  42.8 0.1 collective-permute-start
  42.9 1.5 %collective-permute-done.other_ref = f32[64,8,128]{2,1,0:T(8,128)S(1)} collective-permute-done((f32[64,8,128]{2,1,0:T(8,128)S(1)}, f32[64,8,128]{2,1,0:T(8,128)S(1)}, u32[]{:S(2)}, u32[]{:S(2)}) %collective-permute-start) | collective-permute-done | bytes 262176 | tf_op jit(solution)/shard_map/ppermute | solution.py:406
  44.4 0.0 copy-done.3
  44.4 0.0 copy-done
  44.4 0.0 copy-done.2
  44.5 0.9 %adam.1 = f32[7,8192]{1,0:T(8,128)} custom-call(f32[64,8,128]{2,1,0:T(8,128)S(1)} %scatter.1.own_ref, f32[64,8,128]{2,1,0:T(8,128)S(1)} %collective-permute-done.other_ref, f32[7,8192]{1,0:T(8,128)S(1)} %copy-done, f32[7,8192]{1,0:T(8,128)S(1)} %copy-done.2, f32[7,8192]{1,0:T(8,128)S(1)} %copy-done.3), custom_call_target="tpu_custom_call" | custom-call | tf_op jit(solution)/shard_map/adam/pallas_call | solution.py:410
Async XLA Ops:
  1.8 18.2 %copy-start.1 = (f32[256,256]{1,0:T(8,128)S(1)}, f32[256,256]{1,0:T(8,128)}, u32[]{:S(2)}) copy-start(f32[256,256]{1,0:T(8,128)} %constant.2.clone.table_ref) | copy-start | bytes 786436
  1.9 18.2 %copy-start.4 = (f32[1,1,8,3,256]{4,2,3,1,0:T(8,128)S(1)}, f32[1,1,8,3,256]{4,2,3,1,0:T(8,128)}, u32[]{:S(2)}) copy-start(f32[1,1,8,3,256]{4,2,3,1,0:T(8,128)} %param.16) | copy-start | bytes 73732
  29.3 12.7 %copy-start.5 = (s32[1,1,1,16,4]{3,4,2,1,0:T(4,128)S(1)}, s32[1,1,1,16,4]{3,4,2,1,0:T(4,128)}, u32[]{:S(2)}) copy-start(s32[1,1,1,16,4]{3,4,2,1,0:T(4,128)} %param.13) | copy-start | bytes 772
  29.3 15.2 %copy-start.3 = (f32[7,8192]{1,0:T(8,128)S(1)}, f32[7,8192]{1,0:T(8,128)}, u32[]{:S(2)}) copy-start(f32[7,8192]{1,0:T(8,128)} %two_ref.1) | copy-start | bytes 688132
  42.0 2.4 %copy-start = (f32[7,8192]{1,0:T(8,128)S(1)}, f32[7,8192]{1,0:T(8,128)}, u32[]{:S(2)}) copy-start(f32[7,8192]{1,0:T(8,128)} %params_ref.1) | copy-start | bytes 688132
  42.0 2.4 %copy-start.2 = (f32[7,8192]{1,0:T(8,128)S(1)}, f32[7,8192]{1,0:T(8,128)}, u32[]{:S(2)}) copy-start(f32[7,8192]{1,0:T(8,128)} %one_ref.1) | copy-start | bytes 688132
  42.8 1.6 %collective-permute-start = (f32[64,8,128]{2,1,0:T(8,128)S(1)}, f32[64,8,128]{2,1,0:T(8,128)S(1)}, u32[]{:S(2)}, u32[]{:S(2)}) collective-permute-start(f32[64,8,128]{2,1,0:T(8,128)S(1)} %scatter.1.own_ref), channel_id=1, source_target_pairs={{0,1},{1,0},{2,3},{3,2},{4,5},{5,4},{6,7},{7,6},{8,9},{9,8},{10,11... | collective-permute-start | bytes 786440 | tf_op jit(solution)/shard_map/ppermute | solution.py:406

commit v3 on v2

v3 whole, which is shorter than its diff:
```python
import functools

import jax
import jax.numpy as jnp
import numpy as np
from jax import lax
from jax.experimental import pallas as pl
from jax.experimental.pallas import tpu as pltpu
from jax.sharding import PartitionSpec as P

SIDE = 16
BLOCK = 128
TAPS = 11
PIX = SIDE * SIDE
ROWS = 8
PARAMS = 7

ssim_weight = 0.2
stable_one = 0.0001
stable_two = 0.0009
learn_rate = 0.1
beta_one = 0.9
beta_two = 0.999
adam_eps = 1e-08
first_step = 1
opacity_cap = 0.1
weight_floor = 0.5
f32 = jnp.float32
bf16 = jnp.bfloat16
CHUNK = 16
UNROLL = 32

vmem = pl.BlockSpec(memory_space=pltpu.VMEM)
hbm = pl.BlockSpec(memory_space=pltpu.HBM)


def blur_kron():
    offsets = np.arange(SIDE)[:, None] - np.arange(SIDE)[None, :]
    kernel = np.exp(-(offsets * offsets) / 4.5) * (np.abs(offsets) <= TAPS // 2)
    kernel = kernel / kernel.sum(axis=1, keepdims=True)
    table, parts = np.kron(kernel, kernel).astype(np.float32), []
    for _ in range(3):
        parts.append(table.astype(bf16))
        table = table - parts[-1].astype(np.float32)
    return np.stack(parts)


def pack_kernel(
    block_hbm, anchor_hbm, camera_hbm, params_hbm, items_hbm,
    out_ref, items_ref, row_ref, ids_ref,
    block_ref, anchor_ref, camera_ref, params_ref, sems,
):
    capacity, owners = block_ref.shape
    components = params_ref.shape[0]
    pairs = (
        (params_hbm, params_ref), (block_hbm, block_ref), (anchor_hbm, anchor_ref), (camera_hbm, camera_ref),
        (items_hbm, items_ref), (camera_hbm, row_ref),
    )
    copies = [pltpu.make_async_copy(source, target, sems.at[i]) for i, (source, target) in enumerate(pairs)]
    for copy in copies:
        copy.start()
    for copy in copies:
        copy.wait()
    xx = 1.0 + camera_ref[0, 0]
    xy = camera_ref[0, 1]
    yx = camera_ref[0, 2]
    yy = 1.0 + camera_ref[0, 3]
    slots = owners * capacity
    lane = lax.broadcasted_iota(jnp.int32, ids_ref.shape, 1)
    lane = jnp.where(lane < 3 * slots, lane % slots, -1)
    ids = jnp.full(ids_ref.shape, -1, jnp.int32)
    for index in range(slots):
        owner, slot = index // capacity, index % capacity
        block = block_ref[slot, owner]
        ids = jnp.where(lane == index, block, ids)
        lanes = pl.ds(pl.multiple_of(jnp.maximum(block, 0) * BLOCK, BLOCK), BLOCK)
        tile = params_ref[:, lanes]
        pos_x, pos_y = tile[0:1], tile[1:2]
        row = index * components
        out_ref[row : row + 1, :] = xx * pos_x + xy * pos_y + anchor_ref[0, slot, owner]
        out_ref[row + 1 : row + 2, :] = yx * pos_x + yy * pos_y + anchor_ref[1, slot, owner]
        out_ref[row + 2 : row + components, :] = tile[2:]
    ids_ref[...] = ids


def split_pair(value):
    high = value.astype(bf16)
    return high, (value - high.astype(f32)).astype(bf16)


def precise_dot(value, table_ref, dims):
    rows = value.shape[0]
    parts, rest = [], value
    for _ in range(3):
        parts.append(rest.astype(bf16))
        rest = rest - parts[-1].astype(f32)
    total = None
    for index in range(3):
        left = jnp.concatenate(parts[: 3 - index], axis=0)
        product = lax.dot_general(left, table_ref[index], (dims, ((), ())), preferred_element_type=f32)
        for part in range(3 - index):
            piece = product[part * rows : (part + 1) * rows]
            total = piece if total is None else total + piece
    return total


def padded_rows(values):
    rows = sum(value.shape[0] for value in values)
    extra = -rows % (2 * ROWS)
    if extra:
        values = values + [jnp.zeros((extra, values[0].shape[1]), f32)]
    return jnp.concatenate(values, axis=0)


def owner_kernel(
    items_vmem, camera_vmem, packed_ref, goal_ref, table_ref,
    packed_back_ref, loss_ref,
    items_ref, camera_ref, sems, arrived_ref, back_ref, quant_ref, left_ref, alpha_ref, split_ref, part_ref, diff_ref, mix_ref, grad_ref,
):
    depth, tiles = items_ref.shape
    channels = goal_ref.shape[0]
    count = depth * tiles
    halves = PIX // BLOCK
    slots = arrived_ref.shape[0]
    components = packed_ref.shape[0] // slots
    copies = [
        pltpu.make_async_copy(items_vmem, items_ref, sems.at[0]),
        pltpu.make_async_copy(camera_vmem, camera_ref, sems.at[1]),
    ]
    for copy in copies:
        copy.start()
    back_ref[...] = jnp.zeros_like(back_ref)
    for slot in range(slots):
        kept = min(ROWS, packed_ref.shape[0] - slot * components)
        arrived_ref[slot, 0:kept, :] = packed_ref[slot * components : slot * components + kept, :]
        if kept < ROWS:
            arrived_ref[slot, kept:, :] = jnp.zeros((ROWS - kept, BLOCK), f32)
    goal = jnp.concatenate([goal_ref[ch] for ch in range(channels)], axis=0)
    size = channels * tiles
    blurred_goal = precise_dot(padded_rows([goal, goal * goal]), table_ref, ((1,), (1,)))
    local_b, square_b = blurred_goal[:size], blurred_goal[size : 2 * size]
    for copy in copies:
        copy.wait()
    row8 = lax.broadcasted_iota(jnp.int32, (ROWS, BLOCK), 0)
    places = (lax.broadcasted_iota(jnp.int32, (SIDE, BLOCK), 0).astype(f32) + 0.5) / SIDE

    def forward(index, carry):
        slot = items_ref[index // tiles, index % tiles]
        raw = arrived_ref[slot]
        sig = jax.nn.sigmoid(raw)
        spread = 0.5 * jnp.exp(-2.0 * raw)
        value = jnp.where(row8 < 2, raw, jnp.where(row8 == 2, spread, jnp.where(row8 == 3, opacity_cap * sig, sig)))
        quant_ref[index] = value
        delta_x = places - value[0:1]
        delta_y = places - value[1:2]
        factor_x = jnp.exp(-(delta_x * delta_x) * value[2:3])
        factor_y = value[3:4] * jnp.exp(-(delta_y * delta_y) * value[2:3])
        colour = jnp.where(row8 == 7, 1.0, jnp.where(row8 >= 4, value, 0.0))
        high = colour.astype(bf16).astype(f32)
        low = colour - high
        left = jnp.concatenate([pltpu.roll(low, 5, 0), high + pltpu.roll(high, 4, 0)], axis=0)
        left_ref[index] = left
        left = left.astype(bf16)
        factor_x = jnp.concatenate([factor_x] * (BLOCK // SIDE), axis=0).T
        prods, rights = [], []
        for half in range(halves):
            tall = [
                jnp.broadcast_to(factor_y[half * ROWS + row : half * ROWS + row + 1], (SIDE, BLOCK)) for row in range(ROWS)
            ]
            tall = jnp.concatenate(tall, axis=0).T
            prod, highs, lows = None, [], []
            for chunk in range(BLOCK // CHUNK):
                rows = slice(chunk * CHUNK, (chunk + 1) * CHUNK)
                alpha = factor_x[rows] * tall[rows]
                alpha_ref[index, half, rows, :] = alpha
                high, low = split_pair(alpha)
                split_ref[half, pl.ds(pl.multiple_of(index * BLOCK + chunk * CHUNK, CHUNK), CHUNK), :] = high
                highs.append(high)
                lows.append(low)
                clear = 1.0 - alpha
                prod = clear if prod is None else prod * clear
            prods.append(prod)
            rights.append(jnp.concatenate(highs + lows, axis=0))
        sums = jnp.dot(
            jnp.concatenate([left, left], axis=1), jnp.concatenate(rights, axis=1), preferred_element_type=f32
        )
        sums = sums[ROWS:] + pltpu.roll(sums[:ROWS], ROWS - 1, 0)
        for half in range(halves):
            prod = prods[half][:ROWS] * prods[half][ROWS:]
            for shift in (4, 2, 1):
                prod = prod * pltpu.roll(prod, shift, 0)
            part_ref[half, pl.ds(pl.multiple_of(index * ROWS, ROWS), ROWS), :] = jnp.where(
                row8 == 4, prod, sums[:, half * BLOCK : (half + 1) * BLOCK]
            )
        return carry

    lax.fori_loop(0, count, forward, 0, unroll=UNROLL)

    def gathered(row, rank):
        rows = pl.ds(rank * tiles * ROWS + row, tiles, stride=ROWS)
        return jnp.concatenate([part_ref[half, rows, :] for half in range(halves)], axis=1)

    transmits = [gathered(4, rank) for rank in range(depth)]
    totals = [gathered(3, rank) for rank in range(depth)]
    floors = [jnp.maximum(total, weight_floor) for total in totals]
    ratios = [(1.0 - transmit) / floor for transmit, floor in zip(transmits, floors)]
    weighted = [[gathered(ch, rank) for ch in range(channels)] for rank in range(depth)]
    shaded = [[ratios[rank] * weighted[rank][ch] for ch in range(channels)] for rank in range(depth)]
    fronts = [jnp.ones_like(transmits[0])]
    for rank in range(depth):
        fronts.append(fronts[rank] * transmits[rank])
    images = [sum(fronts[rank] * shaded[rank][ch] for rank in range(depth)) for ch in range(channels)]
    image = jnp.concatenate(images, axis=0)
    blurred = precise_dot(padded_rows([image, image * image, image * goal]), table_ref, ((1,), (1,)))
    local_a, square_a, cross = [blurred[i * size : (i + 1) * size] for i in range(3)]
    var_a = square_a - local_a * local_a
    var_b = square_b - local_b * local_b
    both = cross - local_a * local_b
    top_one = 2.0 * local_a * local_b + stable_one
    top_two = 2.0 * both + stable_two
    low_one = local_a * local_a + local_b * local_b + stable_one
    low_two = var_a + var_b + stable_two
    under = 1.0 / (low_one * low_two)
    similar = top_one * top_two * under
    residue = image - goal
    values = (1.0 - ssim_weight) * residue * residue + ssim_weight * (1.0 - similar)
    per_tile = values[:tiles]
    for ch in range(1, channels):
        per_tile = per_tile + values[ch * tiles : (ch + 1) * tiles]
    norm = 1.0 / (channels * PIX)
    column = jnp.sum(per_tile, axis=1, keepdims=True) * norm
    loss_ref[...] = jnp.broadcast_to(column, (tiles, BLOCK)).T[0:1, :]
    scale = -ssim_weight * norm
    by_top_one = scale * top_two * under
    by_top_two = scale * top_one * under
    by_low_one = -scale * similar / low_one
    by_low_two = -scale * similar / low_two
    by_local = 2.0 * (local_b * (by_top_one - by_top_two) + local_a * (by_low_one - by_low_two))
    spread = precise_dot(padded_rows([by_local, by_low_two, 2.0 * by_top_two]), table_ref, ((1,), (0,)))
    by_image = (
        (2.0 * (1.0 - ssim_weight) * norm) * residue
        + spread[:size] + 2.0 * image * spread[size : 2 * size] + goal * spread[2 * size : 3 * size]
    )
    by_image = [by_image[ch * tiles : (ch + 1) * tiles] for ch in range(channels)]
    diff_ref[...] = jnp.zeros_like(diff_ref)

    def spread_rows(row, rank, value):
        rows = pl.ds(rank * tiles * 2 * ROWS + row, tiles, stride=2 * ROWS)
        for half in range(halves):
            diff_ref[half, rows, :] = value[:, half * BLOCK : (half + 1) * BLOCK]

    by_front = None
    for rank in reversed(range(depth)):
        by_shaded = [fronts[rank] * by_image[ch] for ch in range(channels)]
        by_transmit = -sum(by_shaded[ch] * weighted[rank][ch] for ch in range(channels)) / floors[rank]
        if by_front is not None:
            by_transmit = by_transmit + by_front * fronts[rank]
        own = sum(by_image[ch] * shaded[rank][ch] for ch in range(channels))
        by_front = own if by_front is None else own + by_front * transmits[rank]
        by_floor = -sum(by_shaded[ch] * shaded[rank][ch] for ch in range(channels)) / floors[rank]
        total = totals[rank]
        by_total = by_floor * jnp.where(total > weight_floor, 1.0, jnp.where(total == weight_floor, 0.5, 0.0))
        for q in range(4):
            value = by_shaded[q] * ratios[rank] if q < channels else by_total
            high = value.astype(bf16).astype(f32)
            spread_rows(8 + q, rank, high)
            spread_rows(12 + q, rank, value - high)
            if q < channels:
                spread_rows(1 + q, rank, high)
        spread_rows(0, rank, by_transmit * transmits[rank])

    xx = 1.0 + camera_ref[0, 0]
    xy = camera_ref[0, 1]
    yx = camera_ref[0, 2]
    yy = 1.0 + camera_ref[0, 3]

    group = BLOCK // (2 * ROWS)
    span = group * BLOCK
    places = lax.broadcasted_iota(jnp.int32, (BLOCK, PIX), 1)
    column = lax.broadcasted_iota(jnp.int32, (BLOCK, PIX), 0)
    middle = (SIDE - 1) / 2
    cell_x = (places % SIDE).astype(f32) - middle
    cell_y = (places // SIDE).astype(f32) - middle
    basis = jnp.where(column == ROWS // 2, 1.0, 0.0)
    for free, value in zip((5, 6, 7, 20), (cell_x, cell_y, cell_x * cell_x, cell_y * cell_y)):
        basis = jnp.where(column == free, value, basis)
    basis = basis.astype(bf16)
    basis = jnp.concatenate([basis, basis], axis=1)
    contract = (((1,), (1,)), ((), ()))

    def backward(step):
        block = pl.ds(step * BLOCK, BLOCK)
        wide = pl.ds(step * span, span)
        rows = jnp.concatenate([diff_ref[half, block, :] for half in range(halves)], axis=1).astype(bf16)
        turned = []
        for item in range(group):
            pieces = [left_ref[step * group + item]]
            if item:
                pieces.insert(0, jnp.zeros((item * 2 * ROWS, BLOCK), f32))
            if item < group - 1:
                pieces.append(jnp.zeros(((group - 1 - item) * 2 * ROWS, BLOCK), f32))
            turned.append(jnp.concatenate(pieces, axis=0).T.astype(bf16))
        mix = jnp.dot(jnp.concatenate(turned, axis=0), rows, preferred_element_type=f32)
        for half in range(halves):
            mix_ref[step, half] = mix[:, half * BLOCK : (half + 1) * BLOCK]
        for item in range(group):
            index = step * group + item
            for half in range(halves):
                by_log = diff_ref[half, pl.ds(index * 2 * ROWS, 1), :]
                for chunk in range(BLOCK // CHUNK):
                    alpha = alpha_ref[index, half, chunk * CHUNK : (chunk + 1) * CHUNK, :]
                    inverse = 1.0 / (1.0 - alpha)
                    first = item * BLOCK + chunk * CHUNK
                    grad = alpha * (mix_ref[step, half, first : first + CHUNK, :] - by_log * inverse)
                    high, low = split_pair(grad)
                    grad_ref[step, half, first : first + CHUNK, :] = high
                    grad_ref[step, halves + half, first : first + CHUNK, :] = low
        left = [grad_ref[step, i] for i in range(2 * halves)] + [split_ref[half, wide, :] for half in range(halves)]
        totals = lax.dot_general(
            jnp.concatenate(left, axis=1), jnp.concatenate([basis, rows], axis=1), contract, preferred_element_type=f32
        )
        for item in range(group):
            finish(step * group + item, item, totals[item * BLOCK : (item + 1) * BLOCK].T)

    def finish(index, item, moments):
        slot = items_ref[index // tiles, index % tiles]
        value = quant_ref[index]
        inverse = value[2:3]
        base_x = 0.5 - value[0:1]
        base_y = 0.5 - value[1:2]
        zero, one_x, one_y = moments[4:5], moments[5:6] * (1.0 / SIDE), moments[6:7] * (1.0 / SIDE)
        two = (moments[7:8] + moments[20:21]) * (1.0 / (SIDE * SIDE))
        sum_x = one_x + base_x * zero
        sum_y = one_y + base_y * zero
        sum_r = two + 2.0 * (base_x * one_x + base_y * one_y) + (base_x * base_x + base_y * base_y) * zero
        by_u = 2.0 * inverse * sum_x
        by_w = 2.0 * inverse * sum_y
        back_ref[slot, 0:1, :] = xx * by_u + yx * by_w
        back_ref[slot, 1:2, :] = xy * by_u + yy * by_w
        back_ref[slot, 2:3, :] = 2.0 * inverse * sum_r
        back_ref[slot, 3:4, :] = zero * (1.0 - value[3:4] * (1.0 / opacity_cap))
        shade = value[4:7]
        first = item * 2 * ROWS + ROWS
        back_ref[slot, 4:7, :] = (moments[first : first + 3] + moments[first + 4 : first + 7]) * shade * (1.0 - shade)

    for step in range(count // group):
        backward(step)
    for slot in range(slots):
        packed_back_ref[slot * components : (slot + 1) * components, :] = back_ref[slot, 0:components, :]


def scatter_kernel(ids_ref, grads_ref, out_ref):
    lanes = ids_ref.shape[1]
    components = PARAMS
    slots = grads_ref.shape[0] // components
    blocks = out_ref.shape[0] // components
    block = lax.broadcasted_iota(jnp.int32, (blocks, lanes), 0)
    chosen = jnp.where(block == ids_ref[0:1, :], 1.0, 0.0).astype(bf16)
    columns = []
    for row in range(components):
        rest, parts = grads_ref[pl.ds(row, slots, stride=components), :], []
        for _ in range(3):
            parts.append(rest.astype(bf16))
            rest = rest - parts[-1].astype(f32)
        if lanes > 3 * slots:
            parts.append(jnp.zeros((lanes - 3 * slots, BLOCK), bf16))
        columns.append(jnp.concatenate(parts, axis=0))
    sums = jnp.dot(chosen, jnp.concatenate(columns, axis=1), preferred_element_type=f32)
    for row in range(components):
        out_ref[pl.ds(row, blocks, stride=components), :] = sums[:, row * BLOCK : (row + 1) * BLOCK]


def adam_kernel(own_ref, other_ref, params_ref, one_ref, two_ref, out_ref):
    fix_one = 1.0 - beta_one**first_step
    fix_two = 1.0 - beta_two**first_step
    components = params_ref.shape[0]
    for block in range(params_ref.shape[1] // BLOCK):
        lanes = pl.ds(block * BLOCK, BLOCK)
        rows = slice(block * components, (block + 1) * components)
        grad = own_ref[rows, :]
        if other_ref is not None:
            grad = grad + other_ref[rows, :]
        one = beta_one * one_ref[:, lanes] + (1.0 - beta_one) * grad
        two = beta_two * two_ref[:, lanes] + (1.0 - beta_two) * grad * grad
        out_ref[:, lanes] = params_ref[:, lanes] - learn_rate * (one / fix_one) / (
            jnp.sqrt(two / fix_two) + adam_eps
        )


def limit(size):
    return pltpu.CompilerParams(vmem_limit_bytes=size * 1024 * 1024)


def shards(params, first_moment, second_moment, camera, slot_block, slot_anchor, tile_items, target):
    cells = lax.axis_size("cell")
    views = lax.axis_size("view")
    capacity = slot_block.shape[-1]
    tiles, depth = tile_items.shape[2:]
    channels = target.shape[3]
    per_cell = params.shape[1]
    blocks = per_cell // BLOCK
    slots = cells * capacity
    count = tiles * depth
    halves = PIX // BLOCK
    span = BLOCK // (2 * ROWS) * BLOCK

    camera_row = camera.reshape(1, 4)
    block_ids = jnp.swapaxes(slot_block, 3, 4).reshape(capacity, cells)
    anchors = jnp.swapaxes(slot_anchor, 4, 5).reshape(2, capacity, cells)
    items = jnp.swapaxes(tile_items, 2, 3).reshape(depth, tiles)
    goals = jnp.transpose(target, (0, 1, 3, 2, 4)).reshape(channels, tiles, PIX)
    slab = jax.ShapeDtypeStruct((slots * PARAMS, BLOCK), f32)
    id_lanes = -(-3 * slots // BLOCK) * BLOCK

    def exchange(array):
        array = array.reshape(cells, 1, capacity * PARAMS * BLOCK)
        array = lax.all_to_all(array, "cell", split_axis=0, concat_axis=0, tiled=True)
        return array.reshape(slots * PARAMS, BLOCK)

    packed, items, camera_row, ids = pl.pallas_call(
        pack_kernel,
        out_shape=(slab, jax.ShapeDtypeStruct(items.shape, items.dtype), jax.ShapeDtypeStruct(camera_row.shape, f32),
                   jax.ShapeDtypeStruct((ROWS, id_lanes), jnp.int32)),
        in_specs=[hbm] * 5,
        out_specs=(vmem,) * 4,
        scratch_shapes=[
            pltpu.SMEM(block_ids.shape, jnp.int32),
            pltpu.SMEM(anchors.shape, f32),
            pltpu.SMEM(camera_row.shape, f32),
            pltpu.VMEM(params.shape, f32),
            pltpu.SemaphoreType.DMA((6,)),
        ],
        compiler_params=limit(4),
        name="pack",
    )(*[pltpu.with_memory_space_constraint(array, pltpu.HBM) for array in (block_ids, anchors, camera_row, params, items)])
    arrived = exchange(packed)
    back, losses = pl.pallas_call(
        owner_kernel,
        out_shape=(slab, jax.ShapeDtypeStruct((1, tiles), f32)),
        in_specs=[vmem] * 5,
        out_specs=(vmem, vmem),
        scratch_shapes=[
            pltpu.SMEM(items.shape, jnp.int32),
            pltpu.SMEM(camera_row.shape, f32),
            pltpu.SemaphoreType.DMA((2,)),
            pltpu.VMEM((slots, ROWS, BLOCK), f32),
            pltpu.VMEM((slots, ROWS, BLOCK), f32),
            pltpu.VMEM((count, ROWS, BLOCK), f32),
            pltpu.VMEM((count, 2 * ROWS, BLOCK), f32),
            pltpu.VMEM((count, halves, BLOCK, BLOCK), f32),
            pltpu.VMEM((halves, count * BLOCK, BLOCK), bf16),
            pltpu.VMEM((halves, count * ROWS, BLOCK), f32),
            pltpu.VMEM((halves, count * 2 * ROWS, BLOCK), f32),
            pltpu.VMEM((count * BLOCK // span, halves, span, BLOCK), f32),
            pltpu.VMEM((count * BLOCK // span, 2 * halves, span, BLOCK), bf16),
        ],
        compiler_params=limit(40),
        name="owner",
    )(items, camera_row, arrived, goals, jnp.asarray(blur_kron()))
    returned = exchange(back)
    summed = pl.pallas_call(
        scatter_kernel,
        out_shape=jax.ShapeDtypeStruct((blocks * PARAMS, BLOCK), f32),
        in_specs=[vmem, vmem],
        out_specs=vmem,
        compiler_params=limit(4),
        name="scatter",
    )(ids, returned)
    operands = [summed]
    body = adam_kernel
    if views == 2:
        operands.append(lax.ppermute(summed, "view", [(0, 1), (1, 0)]))
    else:
        operands = [lax.psum(summed, "view")]
        body = lambda own, *rest: adam_kernel(own, None, *rest)
    current = pl.pallas_call(
        body,
        out_shape=jax.ShapeDtypeStruct(params.shape, f32),
        in_specs=[vmem] * (len(operands) + 3),
        out_specs=vmem,
        compiler_params=limit(4),
        name="adam",
    )(*operands, params, first_moment, second_moment)
    return current, losses.reshape(1, 1, tiles)


def solution(mesh):
    placed = (
        P(None, "cell"),
        P(None, "cell"),
        P(None, "cell"),
        P(None, "view", None),
        P(None, "view", "cell", None, None),
        P(None, "view", "cell", None, None, None),
        P(None, "view", "cell", None),
        P(None, "view", "cell", None, None),
    )
    return jax.shard_map(
        shards,
        mesh=mesh,
        in_specs=placed,
        out_specs=(P(None, "cell"), P(None, "view", "cell")),
        check_vma=False,
    )
```

time: 45.6 us -> 40.9 us (0.90)
  Pallas kernels: 12.2 us -> 8.77 us
  blocking collectives: 30.9 us -> 29.6 us
    pallas_call x1, Pallas kernels: 9.27 us -> 6.43 us  [shards(): pl.pallas_call(owner_kernel, out_shape=(slab, jax.ShapeDtypeStruct((1, ti...]
    all_to_all x2, blocking collectives: 30.9 us -> 29.6 us  [exchange(): lax.all_to_all(array, 'cell', split_axis=0, concat_axis=0, tiled=True)]
    pallas_call x1, Pallas kernels: 0.81 us -> 0.18 us  [shards(): pl.pallas_call(scatter_kernel, out_shape=jax.ShapeDtypeStruct((blocks * P...]
where the time goes in v3:
time: 40.9 us; the launch traced here: 40.6 us
  blocking collectives  29.6 us (72%)
  Pallas kernels  8.77 us (21%)
  waiting for transfers between devices  1.48 us (4%)
  between operations  0.7 us (2%)
    all_to_all x2, blocking collectives, exchange(): lax.all_to_all(array, 'cell', split_axis=0, concat_axis=0, tiled=True)  29.6 us
    pallas_call x1, Pallas kernels, shards(): pl.pallas_call(owner_kernel, out_shape=(slab, jax.ShapeDtypeStruct((1, ti...  6.43 us
    ppermute x1, waiting for transfers between devices, shards(): operands.append(lax.ppermute(summed, 'view', [(0, 1), (1, 0)]))  1.48 us
    pallas_call x1, Pallas kernels, shards(): pl.pallas_call(pack_kernel, out_shape=(slab, jax.ShapeDtypeStruct(items.s...  1.25 us
    pallas_call x1, Pallas kernels, shards(): pl.pallas_call(body, out_shape=jax.ShapeDtypeStruct(params.shape, f32), i...  0.9 us
  transfers between devices with their start and end apart: 1, of which 1 were waited for; matrix products, arithmetic and copies ran while one was open for 0% of the time, Pallas kernels for 0%

profile of v3, /device:TPU:0, one launch (start us, length us, event | category | flops | bytes accessed | tf_op | source)
XLA Modules:
  0.0 40.6 jit_solution(7055025746290772861)
XLA Ops:
  0.6 0.0 copy-start.1
  0.6 1.3 %pack.1 = (f32[448,128]{1,0:T(8,128)S(1)}, s32[4,8]{1,0:T(4,128)S(1)}, f32[1,4]{1,0:T(1,128)S(1)}, s32[8,256]{1,0:T(8,128)S(1)}) custom-call(s32[4,16]{1,0:T(4,128)} %bitcast.24, f32[2,4,16]{2,1,0:T(4,128)} %bitcast.23, f32[1,4]{1,0:T(1,128)} %bitcast.26, f32[7,8192]{1,0:T(8,128)} %params_ref.1, s32[4,8]{1,0:T(4,128)} %bitcast.25), custom_call_target="tpu_custom_call" | custom-call | tf_op jit(solution)/shard_map/pack/pallas_call | solution.py:420
  1.9 0.0 copy-start.4
  1.9 17.4 %all_to_all.10 = f32[16,1,3584]{2,1,0:T(1,128)S(1)} all-to-all(f32[16,1,3584]{2,1,0:T(1,128)S(1)} %bitcast.21), channel_id=1, replica_groups=mesh['cell'=16,'view'=2] {'cell'}, dimensions={0} | all-to-all | bytes 458752 | tf_op jit(solution)/shard_map/all_to_all | solution.py:417
  19.3 0.0 copy-done.1
  19.3 0.0 copy-done.4
  19.3 6.4 %owner.1 = (f32[448,128]{1,0:T(8,128)S(1)}, f32[1,8]{1,0:T(1,128)}) custom-call(s32[4,8]{1,0:T(4,128)S(1)} %get-tuple-element.9.items_vmem, f32[1,4]{1,0:T(1,128)S(1)} %get-tuple-element.10.camera_vmem, f32[448,128]{1,0:T(8,128)S(1)} %bitcast.19, f32[3,8,256]{2,1,0:T(8,128)S(1)} %bitcast.22, bf16[3,256,256]{2,1,0:T(8,128)(2,1)S(1)} %copy-done.1), custom_call_target="tpu_custom_call" | custom-call | tf_op jit(solution)/shard_map/owner/pallas_call | solution.py:437
  25.8 0.0 copy-start.2
  25.8 0.0 copy-start.3
  25.8 12.2 %all_to_all.11 = f32[16,1,3584]{2,1,0:T(1,128)S(1)} all-to-all(f32[16,1,3584]{2,1,0:T(1,128)S(1)} %bitcast.20), channel_id=1, replica_groups=mesh['cell'=16,'view'=2] {'cell'}, dimensions={0} | all-to-all | bytes 458752 | tf_op jit(solution)/shard_map/all_to_all | solution.py:417
  37.9 0.0 copy-start
  37.9 0.2 scatter.1.own_ref
  38.1 0.1 collective-permute-start
  38.2 1.5 %collective-permute-done.other_ref = f32[448,128]{1,0:T(8,128)S(1)} collective-permute-done((f32[448,128]{1,0:T(8,128)S(1)}, f32[448,128]{1,0:T(8,128)S(1)}, u32[]{:S(2)}, u32[]{:S(2)}) %collective-permute-start) | collective-permute-done | bytes 229408 | tf_op jit(solution)/shard_map/ppermute | solution.py:472
  39.7 0.0 copy-done.2
  39.7 0.0 copy-done.3
  39.7 0.0 copy-done
  39.7 0.9 %adam.1 = f32[7,8192]{1,0:T(8,128)} custom-call(f32[448,128]{1,0:T(8,128)S(1)} %scatter.1.own_ref, f32[448,128]{1,0:T(8,128)S(1)} %collective-permute-done.other_ref, f32[7,8192]{1,0:T(8,128)S(1)} %copy-done, f32[7,8192]{1,0:T(8,128)S(1)} %copy-done.2, f32[7,8192]{1,0:T(8,128)S(1)} %copy-done.3), custom_call_target="tpu_custom_call" | custom-call | tf_op jit(solution)/shard_map/adam/pallas_call | solution.py:476
Async XLA Ops:
  0.6 18.7 %copy-start.1 = (bf16[3,256,256]{2,1,0:T(8,128)(2,1)S(1)}, bf16[3,256,256]{2,1,0:T(8,128)(2,1)}, u32[]{:S(2)}) copy-start(bf16[3,256,256]{2,1,0:T(8,128)(2,1)} %constant.2.clone.table_ref) | copy-start | bytes 1179652
  1.9 17.4 %copy-start.4 = (f32[1,1,8,3,256]{4,2,3,1,0:T(8,128)S(1)}, f32[1,1,8,3,256]{4,2,3,1,0:T(8,128)}, u32[]{:S(2)}) copy-start(f32[1,1,8,3,256]{4,2,3,1,0:T(8,128)} %param.16) | copy-start | bytes 73732
  25.8 13.9 %copy-start.2 = (f32[7,8192]{1,0:T(8,128)S(1)}, f32[7,8192]{1,0:T(8,128)}, u32[]{:S(2)}) copy-start(f32[7,8192]{1,0:T(8,128)} %one_ref.1) | copy-start | bytes 688132
  25.8 13.9 %copy-start.3 = (f32[7,8192]{1,0:T(8,128)S(1)}, f32[7,8192]{1,0:T(8,128)}, u32[]{:S(2)}) copy-start(f32[7,8192]{1,0:T(8,128)} %two_ref.1) | copy-start | bytes 688132
  37.9 1.8 %copy-start = (f32[7,8192]{1,0:T(8,128)S(1)}, f32[7,8192]{1,0:T(8,128)}, u32[]{:S(2)}) copy-start(f32[7,8192]{1,0:T(8,128)} %params_ref.1) | copy-start | bytes 688132
  38.1 1.6 %collective-permute-start = (f32[448,128]{1,0:T(8,128)S(1)}, f32[448,128]{1,0:T(8,128)S(1)}, u32[]{:S(2)}, u32[]{:S(2)}) collective-permute-start(f32[448,128]{1,0:T(8,128)S(1)} %scatter.1.own_ref), channel_id=1, source_target_pairs={{0,1},{1,0},{2,3},{3,2},{4,5},{5,4},{6,7},{7,6},{8,9},{9,8},{10,11... | collective-permute-start | bytes 688136 | tf_op jit(solution)/shard_map/ppermute | solution.py:472

commit v4 on v3

--- a/solution.py
+++ b/solution.py
@@ -59,7 +59,7 @@
     copies = [pltpu.make_async_copy(source, target, sems.at[i]) for i, (source, target) in enumerate(pairs)]
     for copy in copies:
         copy.start()
-    for copy in copies:
+    for copy in copies[1:]:
         copy.wait()
     xx = 1.0 + camera_ref[0, 0]
     xy = camera_ref[0, 1]
@@ -70,9 +70,12 @@
     lane = jnp.where(lane < 3 * slots, lane % slots, -1)
     ids = jnp.full(ids_ref.shape, -1, jnp.int32)
     for index in range(slots):
+        ids = jnp.where(lane == index, block_ref[index % capacity, index // capacity], ids)
+    ids_ref[...] = ids
+    copies[0].wait()
+    for index in range(slots):
         owner, slot = index // capacity, index % capacity
         block = block_ref[slot, owner]
-        ids = jnp.where(lane == index, block, ids)
         lanes = pl.ds(pl.multiple_of(jnp.maximum(block, 0) * BLOCK, BLOCK), BLOCK)
         tile = params_ref[:, lanes]
         pos_x, pos_y = tile[0:1], tile[1:2]
@@ -80,7 +83,6 @@
         out_ref[row : row + 1, :] = xx * pos_x + xy * pos_y + anchor_ref[0, slot, owner]
         out_ref[row + 1 : row + 2, :] = yx * pos_x + yy * pos_y + anchor_ref[1, slot, owner]
         out_ref[row + 2 : row + components, :] = tile[2:]
-    ids_ref[...] = ids
 
 
 def split_pair(value):
@@ -114,8 +116,8 @@
 
 def owner_kernel(
     items_vmem, camera_vmem, packed_ref, goal_ref, table_ref,
-    packed_back_ref, loss_ref,
-    items_ref, camera_ref, sems, arrived_ref, back_ref, quant_ref, left_ref, alpha_ref, split_ref, part_ref, diff_ref, mix_ref, grad_ref,
+    packed_back_ref, loss_hbm,
+    items_ref, camera_ref, loss_ref, sems, arrived_ref, back_ref, quant_ref, left_ref, alpha_ref, split_ref, part_ref, diff_ref,
 ):
     depth, tiles = items_ref.shape
     channels = goal_ref.shape[0]
@@ -230,6 +232,8 @@
     norm = 1.0 / (channels * PIX)
     column = jnp.sum(per_tile, axis=1, keepdims=True) * norm
     loss_ref[...] = jnp.broadcast_to(column, (tiles, BLOCK)).T[0:1, :]
+    loss_copy = pltpu.make_async_copy(loss_ref, loss_hbm, sems.at[2])
+    loss_copy.start()
     scale = -ssim_weight * norm
     by_top_one = scale * top_two * under
     by_top_two = scale * top_one * under
@@ -288,21 +292,19 @@
     basis = jnp.concatenate([basis, basis], axis=1)
     contract = (((1,), (1,)), ((), ()))
 
-    def backward(step):
+    owner_lane = lax.broadcasted_iota(jnp.int32, (BLOCK, BLOCK), 1) // (2 * ROWS)
+
+    def mixed(step):
         block = pl.ds(step * BLOCK, BLOCK)
-        wide = pl.ds(step * span, span)
         rows = jnp.concatenate([diff_ref[half, block, :] for half in range(halves)], axis=1).astype(bf16)
-        turned = []
-        for item in range(group):
-            pieces = [left_ref[step * group + item]]
-            if item:
-                pieces.insert(0, jnp.zeros((item * 2 * ROWS, BLOCK), f32))
-            if item < group - 1:
-                pieces.append(jnp.zeros(((group - 1 - item) * 2 * ROWS, BLOCK), f32))
-            turned.append(jnp.concatenate(pieces, axis=0).T.astype(bf16))
+        lefts = [left_ref[step * group + item] for item in range(group)]
+        turned = jnp.concatenate(lefts, axis=0).T
+        turned = [jnp.where(owner_lane == item, turned, 0.0).astype(bf16) for item in range(group)]
         mix = jnp.dot(jnp.concatenate(turned, axis=0), rows, preferred_element_type=f32)
-        for half in range(halves):
-            mix_ref[step, half] = mix[:, half * BLOCK : (half + 1) * BLOCK]
+        return rows, mix
+
+    def gradients(step, mix):
+        found = [[] for _ in range(2 * halves)]
         for item in range(group):
             index = step * group + item
             for half in range(halves):
@@ -311,14 +313,20 @@
                     alpha = alpha_ref[index, half, chunk * CHUNK : (chunk + 1) * CHUNK, :]
                     inverse = 1.0 / (1.0 - alpha)
                     first = item * BLOCK + chunk * CHUNK
-                    grad = alpha * (mix_ref[step, half, first : first + CHUNK, :] - by_log * inverse)
+                    grad = alpha * (mix[first : first + CHUNK, half * BLOCK : (half + 1) * BLOCK] - by_log * inverse)
                     high, low = split_pair(grad)
-                    grad_ref[step, half, first : first + CHUNK, :] = high
-                    grad_ref[step, halves + half, first : first + CHUNK, :] = low
-        left = [grad_ref[step, i] for i in range(2 * halves)] + [split_ref[half, wide, :] for half in range(halves)]
-        totals = lax.dot_general(
+                    found[half].append(high)
+                    found[halves + half].append(low)
+        return [jnp.concatenate(pieces, axis=0) for pieces in found]
+
+    def moments_of(step, rows, left):
+        wide = pl.ds(step * span, span)
+        left = left + [split_ref[half, wide, :] for half in range(halves)]
+        return lax.dot_general(
             jnp.concatenate(left, axis=1), jnp.concatenate([basis, rows], axis=1), contract, preferred_element_type=f32
         )
+
+    def finished(step, totals):
         for item in range(group):
             finish(step * group + item, item, totals[item * BLOCK : (item + 1) * BLOCK].T)
 
@@ -343,10 +351,20 @@
         first = item * 2 * ROWS + ROWS
         back_ref[slot, 4:7, :] = (moments[first : first + 3] + moments[first + 4 : first + 7]) * shade * (1.0 - shade)
 
-    for step in range(count // group):
-        backward(step)
+    steps = count // group
+    rows = [mixed(0)]
+    waiting = None
+    for step in range(steps):
+        if step + 1 < steps:
+            rows.append(mixed(step + 1))
+        totals = moments_of(step, rows[step][0], gradients(step, rows[step][1]))
+        if waiting is not None:
+            finished(step - 1, waiting)
+        waiting = totals
+    finished(steps - 1, waiting)
     for slot in range(slots):
         packed_back_ref[slot * components : (slot + 1) * components, :] = back_ref[slot, 0:components, :]
+    loss_copy.wait()
 
 
 def scatter_kernel(ids_ref, grads_ref, out_ref):
@@ -370,21 +388,30 @@
         out_ref[pl.ds(row, blocks, stride=components), :] = sums[:, row * BLOCK : (row + 1) * BLOCK]
 
 
-def adam_kernel(own_ref, other_ref, params_ref, one_ref, two_ref, out_ref):
+def adam_kernel(own_ref, other_ref, params_ref, one_ref, two_ref, out_hbm, out_ref, sems):
     fix_one = 1.0 - beta_one**first_step
     fix_two = 1.0 - beta_two**first_step
     components = params_ref.shape[0]
-    for block in range(params_ref.shape[1] // BLOCK):
-        lanes = pl.ds(block * BLOCK, BLOCK)
-        rows = slice(block * components, (block + 1) * components)
-        grad = own_ref[rows, :]
-        if other_ref is not None:
-            grad = grad + other_ref[rows, :]
-        one = beta_one * one_ref[:, lanes] + (1.0 - beta_one) * grad
-        two = beta_two * two_ref[:, lanes] + (1.0 - beta_two) * grad * grad
-        out_ref[:, lanes] = params_ref[:, lanes] - learn_rate * (one / fix_one) / (
-            jnp.sqrt(two / fix_two) + adam_eps
-        )
+    chunks = sems.shape[0]
+    width = params_ref.shape[1] // chunks
+    copies = []
+    for chunk in range(chunks):
+        for block in range(chunk * width // BLOCK, (chunk + 1) * width // BLOCK):
+            lanes = pl.ds(block * BLOCK, BLOCK)
+            rows = slice(block * components, (block + 1) * components)
+            grad = own_ref[rows, :]
+            if other_ref is not None:
+                grad = grad + other_ref[rows, :]
+            one = beta_one * one_ref[:, lanes] + (1.0 - beta_one) * grad
+            two = beta_two * two_ref[:, lanes] + (1.0 - beta_two) * grad * grad
+            out_ref[:, lanes] = params_ref[:, lanes] - learn_rate * (one / fix_one) / (
+                jnp.sqrt(two / fix_two) + adam_eps
+            )
+        lanes = pl.ds(chunk * width, width)
+        copies.append(pltpu.make_async_copy(out_ref.at[:, lanes], out_hbm.at[:, lanes], sems.at[chunk]))
+        copies[-1].start()
+    for copy in copies:
+        copy.wait()
 
 
 def limit(size):
@@ -402,7 +429,6 @@
     slots = cells * capacity
     count = tiles * depth
     halves = PIX // BLOCK
-    span = BLOCK // (2 * ROWS) * BLOCK
 
     camera_row = camera.reshape(1, 4)
     block_ids = jnp.swapaxes(slot_block, 3, 4).reshape(capacity, cells)
@@ -438,11 +464,12 @@
         owner_kernel,
         out_shape=(slab, jax.ShapeDtypeStruct((1, tiles), f32)),
         in_specs=[vmem] * 5,
-        out_specs=(vmem, vmem),
+        out_specs=(vmem, hbm),
         scratch_shapes=[
             pltpu.SMEM(items.shape, jnp.int32),
             pltpu.SMEM(camera_row.shape, f32),
-            pltpu.SemaphoreType.DMA((2,)),
+            pltpu.VMEM((1, tiles), f32),
+            pltpu.SemaphoreType.DMA((3,)),
             pltpu.VMEM((slots, ROWS, BLOCK), f32),
             pltpu.VMEM((slots, ROWS, BLOCK), f32),
             pltpu.VMEM((count, ROWS, BLOCK), f32),
@@ -451,8 +478,6 @@
             pltpu.VMEM((halves, count * BLOCK, BLOCK), bf16),
             pltpu.VMEM((halves, count * ROWS, BLOCK), f32),
             pltpu.VMEM((halves, count * 2 * ROWS, BLOCK), f32),
-            pltpu.VMEM((count * BLOCK // span, halves, span, BLOCK), f32),
-            pltpu.VMEM((count * BLOCK // span, 2 * halves, span, BLOCK), bf16),
         ],
         compiler_params=limit(40),
         name="owner",
@@ -477,7 +502,8 @@
         body,
         out_shape=jax.ShapeDtypeStruct(params.shape, f32),
         in_specs=[vmem] * (len(operands) + 3),
-        out_specs=vmem,
+        out_specs=hbm,
+        scratch_shapes=[pltpu.VMEM(params.shape, f32), pltpu.SemaphoreType.DMA((4,))],
         compiler_params=limit(4),
         name="adam",
     )(*operands, params, first_moment, second_moment)

time: 40.9 us -> 40.6 us (level)
  no operation moved by 1% of the time
where the time goes in v4:
time: 40.6 us; the launch traced here: 40.3 us
  blocking collectives  29.5 us (73%)
  Pallas kernels  8.5 us (21%)
  waiting for transfers between devices  1.48 us (4%)
  between operations  0.7 us (2%)
    all_to_all x2, blocking collectives, exchange(): lax.all_to_all(array, 'cell', split_axis=0, concat_axis=0, tiled=True)  29.5 us
    pallas_call x1, Pallas kernels, shards(): pl.pallas_call(owner_kernel, out_shape=(slab, jax.ShapeDtypeStruct((1, ti...  6.24 us
    ppermute x1, waiting for transfers between devices, shards(): operands.append(lax.ppermute(summed, 'view', [(0, 1), (1, 0)]))  1.48 us
    pallas_call x1, Pallas kernels, shards(): pl.pallas_call(pack_kernel, out_shape=(slab, jax.ShapeDtypeStruct(items.s...  1.21 us
    pallas_call x1, Pallas kernels, shards(): pl.pallas_call(body, out_shape=jax.ShapeDtypeStruct(params.shape, f32), i...  0.86 us
  transfers between devices with their start and end apart: 1, of which 1 were waited for; matrix products, arithmetic and copies ran while one was open for 0% of the time, Pallas kernels for 0%

profile of v4, /device:TPU:0, one launch (start us, length us, event | category | flops | bytes accessed | tf_op | source)
XLA Modules:
  0.0 40.3 jit_solution(5416601187945325565)
XLA Ops:
  0.6 0.0 copy-start.1
  0.6 1.2 %pack.1 = (f32[448,128]{1,0:T(8,128)S(1)}, s32[4,8]{1,0:T(4,128)S(1)}, f32[1,4]{1,0:T(1,128)S(1)}, s32[8,256]{1,0:T(8,128)S(1)}) custom-call(s32[4,16]{1,0:T(4,128)} %bitcast.24, f32[2,4,16]{2,1,0:T(4,128)} %bitcast.23, f32[1,4]{1,0:T(1,128)} %bitcast.26, f32[7,8192]{1,0:T(8,128)} %params_ref.1, s32[4,8]{1,0:T(4,128)} %bitcast.25), custom_call_target="tpu_custom_call" | custom-call | tf_op jit(solution)/shard_map/pack/pallas_call | solution.py:446
  1.9 0.0 copy-start.4
  1.9 17.4 %all_to_all.10 = f32[16,1,3584]{2,1,0:T(1,128)S(1)} all-to-all(f32[16,1,3584]{2,1,0:T(1,128)S(1)} %bitcast.21), channel_id=1, replica_groups=mesh['cell'=16,'view'=2] {'cell'}, dimensions={0} | all-to-all | bytes 458752 | tf_op jit(solution)/shard_map/all_to_all | solution.py:443
  19.3 0.0 copy-done.1
  19.3 0.0 copy-done.4
  19.3 6.2 %owner.1 = (f32[448,128]{1,0:T(8,128)S(1)}, f32[1,8]{1,0:T(1,128)}) custom-call(s32[4,8]{1,0:T(4,128)S(1)} %get-tuple-element.9.items_vmem, f32[1,4]{1,0:T(1,128)S(1)} %get-tuple-element.10.camera_vmem, f32[448,128]{1,0:T(8,128)S(1)} %bitcast.19, f32[3,8,256]{2,1,0:T(8,128)S(1)} %bitcast.22, bf16[3,256,256]{2,1,0:T(8,128)(2,1)S(1)} %copy-done.1), custom_call_target="tpu_custom_call" | custom-call | tf_op jit(solution)/shard_map/owner/pallas_call | solution.py:463
  25.5 0.0 copy-start.2
  25.5 0.0 copy-start.3
  25.5 12.1 %all_to_all.11 = f32[16,1,3584]{2,1,0:T(1,128)S(1)} all-to-all(f32[16,1,3584]{2,1,0:T(1,128)S(1)} %bitcast.20), channel_id=1, replica_groups=mesh['cell'=16,'view'=2] {'cell'}, dimensions={0} | all-to-all | bytes 458752 | tf_op jit(solution)/shard_map/all_to_all | solution.py:443
  37.7 0.0 copy-start
  37.7 0.2 scatter.1.own_ref
  37.9 0.1 collective-permute-start
  38.0 1.5 %collective-permute-done.other_ref = f32[448,128]{1,0:T(8,128)S(1)} collective-permute-done((f32[448,128]{1,0:T(8,128)S(1)}, f32[448,128]{1,0:T(8,128)S(1)}, u32[]{:S(2)}, u32[]{:S(2)}) %collective-permute-start) | collective-permute-done | bytes 229408 | tf_op jit(solution)/shard_map/ppermute | solution.py:497
  39.4 0.0 copy-done.2
  39.4 0.0 copy-done.3
  39.5 0.0 copy-done
  39.5 0.9 %adam.1 = f32[7,8192]{1,0:T(8,128)} custom-call(f32[448,128]{1,0:T(8,128)S(1)} %scatter.1.own_ref, f32[448,128]{1,0:T(8,128)S(1)} %collective-permute-done.other_ref, f32[7,8192]{1,0:T(8,128)S(1)} %copy-done, f32[7,8192]{1,0:T(8,128)S(1)} %copy-done.2, f32[7,8192]{1,0:T(8,128)S(1)} %copy-done.3), custom_call_target="tpu_custom_call" | custom-call | tf_op jit(solution)/shard_map/adam/pallas_call | solution.py:501
Async XLA Ops:
  0.6 18.6 %copy-start.1 = (bf16[3,256,256]{2,1,0:T(8,128)(2,1)S(1)}, bf16[3,256,256]{2,1,0:T(8,128)(2,1)}, u32[]{:S(2)}) copy-start(bf16[3,256,256]{2,1,0:T(8,128)(2,1)} %constant.2.clone.table_ref) | copy-start | bytes 1179652
  1.9 17.4 %copy-start.4 = (f32[1,1,8,3,256]{4,2,3,1,0:T(8,128)S(1)}, f32[1,1,8,3,256]{4,2,3,1,0:T(8,128)}, u32[]{:S(2)}) copy-start(f32[1,1,8,3,256]{4,2,3,1,0:T(8,128)} %param.16) | copy-start | bytes 73732
  25.5 13.9 %copy-start.2 = (f32[7,8192]{1,0:T(8,128)S(1)}, f32[7,8192]{1,0:T(8,128)}, u32[]{:S(2)}) copy-start(f32[7,8192]{1,0:T(8,128)} %one_ref.1) | copy-start | bytes 688132
  25.5 13.9 %copy-start.3 = (f32[7,8192]{1,0:T(8,128)S(1)}, f32[7,8192]{1,0:T(8,128)}, u32[]{:S(2)}) copy-start(f32[7,8192]{1,0:T(8,128)} %two_ref.1) | copy-start | bytes 688132
  37.7 1.8 %copy-start = (f32[7,8192]{1,0:T(8,128)S(1)}, f32[7,8192]{1,0:T(8,128)}, u32[]{:S(2)}) copy-start(f32[7,8192]{1,0:T(8,128)} %params_ref.1) | copy-start | bytes 688132
  37.9 1.6 %collective-permute-start = (f32[448,128]{1,0:T(8,128)S(1)}, f32[448,128]{1,0:T(8,128)S(1)}, u32[]{:S(2)}, u32[]{:S(2)}) collective-permute-start(f32[448,128]{1,0:T(8,128)S(1)} %scatter.1.own_ref), channel_id=1, source_target_pairs={{0,1},{1,0},{2,3},{3,2},{4,5},{5,4},{6,7},{7,6},{8,9},{9,8},{10,11... | collective-permute-start | bytes 688136 | tf_op jit(solution)/shard_map/ppermute | solution.py:497

commit v5 on v4

--- a/solution.py
+++ b/solution.py
@@ -132,26 +132,27 @@
     for copy in copies:
         copy.start()
     back_ref[...] = jnp.zeros_like(back_ref)
+    row8 = lax.broadcasted_iota(jnp.int32, (ROWS, BLOCK), 0)
     for slot in range(slots):
         kept = min(ROWS, packed_ref.shape[0] - slot * components)
         arrived_ref[slot, 0:kept, :] = packed_ref[slot * components : slot * components + kept, :]
         if kept < ROWS:
             arrived_ref[slot, kept:, :] = jnp.zeros((ROWS - kept, BLOCK), f32)
+        raw = arrived_ref[slot]
+        sig = jax.nn.sigmoid(raw)
+        spread = 0.5 * jnp.exp(-2.0 * raw)
+        arrived_ref[slot] = jnp.where(row8 < 2, raw, jnp.where(row8 == 2, spread, jnp.where(row8 == 3, opacity_cap * sig, sig)))
     goal = jnp.concatenate([goal_ref[ch] for ch in range(channels)], axis=0)
     size = channels * tiles
     blurred_goal = precise_dot(padded_rows([goal, goal * goal]), table_ref, ((1,), (1,)))
     local_b, square_b = blurred_goal[:size], blurred_goal[size : 2 * size]
     for copy in copies:
         copy.wait()
-    row8 = lax.broadcasted_iota(jnp.int32, (ROWS, BLOCK), 0)
     places = (lax.broadcasted_iota(jnp.int32, (SIDE, BLOCK), 0).astype(f32) + 0.5) / SIDE
 
     def forward(index, carry):
         slot = items_ref[index // tiles, index % tiles]
-        raw = arrived_ref[slot]
-        sig = jax.nn.sigmoid(raw)
-        spread = 0.5 * jnp.exp(-2.0 * raw)
-        value = jnp.where(row8 < 2, raw, jnp.where(row8 == 2, spread, jnp.where(row8 == 3, opacity_cap * sig, sig)))
+        value = arrived_ref[slot]
         quant_ref[index] = value
         delta_x = places - value[0:1]
         delta_y = places - value[1:2]

time: 40.6 us -> 40.6 us (level)
  no operation moved by 1% of the time
where the time goes in v5:
time: 40.6 us; the launch traced here: 40.3 us
  blocking collectives  29.5 us (73%)
  Pallas kernels  8.5 us (21%)
  waiting for transfers between devices  1.48 us (4%)
  between operations  0.7 us (2%)
    all_to_all x2, blocking collectives, exchange(): lax.all_to_all(array, 'cell', split_axis=0, concat_axis=0, tiled=True)  29.5 us
    pallas_call x1, Pallas kernels, shards(): pl.pallas_call(owner_kernel, out_shape=(slab, jax.ShapeDtypeStruct((1, ti...  6.24 us
    ppermute x1, waiting for transfers between devices, shards(): operands.append(lax.ppermute(summed, 'view', [(0, 1), (1, 0)]))  1.48 us
    pallas_call x1, Pallas kernels, shards(): pl.pallas_call(pack_kernel, out_shape=(slab, jax.ShapeDtypeStruct(items.s...  1.21 us
    pallas_call x1, Pallas kernels, shards(): pl.pallas_call(body, out_shape=jax.ShapeDtypeStruct(params.shape, f32), i...  0.86 us
  transfers between devices with their start and end apart: 1, of which 1 were waited for; matrix products, arithmetic and copies ran while one was open for 0% of the time, Pallas kernels for 0%

profile of v5, /device:TPU:0, one launch (start us, length us, event | category | flops | bytes accessed | tf_op | source)
XLA Modules:
  0.0 40.3 jit_solution(6586688098319218991)
XLA Ops:
  0.6 0.0 copy-start.1
  0.6 1.2 %pack.1 = (f32[448,128]{1,0:T(8,128)S(1)}, s32[4,8]{1,0:T(4,128)S(1)}, f32[1,4]{1,0:T(1,128)S(1)}, s32[8,256]{1,0:T(8,128)S(1)}) custom-call(s32[4,16]{1,0:T(4,128)} %bitcast.24, f32[2,4,16]{2,1,0:T(4,128)} %bitcast.23, f32[1,4]{1,0:T(1,128)} %bitcast.26, f32[7,8192]{1,0:T(8,128)} %params_ref.1, s32[4,8]{1,0:T(4,128)} %bitcast.25), custom_call_target="tpu_custom_call" | custom-call | tf_op jit(solution)/shard_map/pack/pallas_call | solution.py:447
  1.9 0.0 copy-start.4
  1.9 17.4 %all_to_all.10 = f32[16,1,3584]{2,1,0:T(1,128)S(1)} all-to-all(f32[16,1,3584]{2,1,0:T(1,128)S(1)} %bitcast.21), channel_id=1, replica_groups=mesh['cell'=16,'view'=2] {'cell'}, dimensions={0} | all-to-all | bytes 458752 | tf_op jit(solution)/shard_map/all_to_all | solution.py:444
  19.3 0.0 copy-done.1
  19.3 0.0 copy-done.4
  19.3 6.2 %owner.1 = (f32[448,128]{1,0:T(8,128)S(1)}, f32[1,8]{1,0:T(1,128)}) custom-call(s32[4,8]{1,0:T(4,128)S(1)} %get-tuple-element.9.items_vmem, f32[1,4]{1,0:T(1,128)S(1)} %get-tuple-element.10.camera_vmem, f32[448,128]{1,0:T(8,128)S(1)} %bitcast.19, f32[3,8,256]{2,1,0:T(8,128)S(1)} %bitcast.22, bf16[3,256,256]{2,1,0:T(8,128)(2,1)S(1)} %copy-done.1), custom_call_target="tpu_custom_call" | custom-call | tf_op jit(solution)/shard_map/owner/pallas_call | solution.py:464
  25.5 0.0 copy-start.2
  25.5 0.0 copy-start.3
  25.6 12.1 %all_to_all.11 = f32[16,1,3584]{2,1,0:T(1,128)S(1)} all-to-all(f32[16,1,3584]{2,1,0:T(1,128)S(1)} %bitcast.20), channel_id=1, replica_groups=mesh['cell'=16,'view'=2] {'cell'}, dimensions={0} | all-to-all | bytes 458752 | tf_op jit(solution)/shard_map/all_to_all | solution.py:444
  37.7 0.0 copy-start
  37.7 0.2 scatter.1.own_ref
  37.9 0.1 collective-permute-start
  38.0 1.5 %collective-permute-done.other_ref = f32[448,128]{1,0:T(8,128)S(1)} collective-permute-done((f32[448,128]{1,0:T(8,128)S(1)}, f32[448,128]{1,0:T(8,128)S(1)}, u32[]{:S(2)}, u32[]{:S(2)}) %collective-permute-start) | collective-permute-done | bytes 229408 | tf_op jit(solution)/shard_map/ppermute | solution.py:498
  39.5 0.0 copy-done.2
  39.5 0.0 copy-done.3
  39.5 0.0 copy-done
  39.5 0.9 %adam.1 = f32[7,8192]{1,0:T(8,128)} custom-call(f32[448,128]{1,0:T(8,128)S(1)} %scatter.1.own_ref, f32[448,128]{1,0:T(8,128)S(1)} %collective-permute-done.other_ref, f32[7,8192]{1,0:T(8,128)S(1)} %copy-done, f32[7,8192]{1,0:T(8,128)S(1)} %copy-done.2, f32[7,8192]{1,0:T(8,128)S(1)} %copy-done.3), custom_call_target="tpu_custom_call" | custom-call | tf_op jit(solution)/shard_map/adam/pallas_call | solution.py:502
Async XLA Ops:
  0.6 18.6 %copy-start.1 = (bf16[3,256,256]{2,1,0:T(8,128)(2,1)S(1)}, bf16[3,256,256]{2,1,0:T(8,128)(2,1)}, u32[]{:S(2)}) copy-start(bf16[3,256,256]{2,1,0:T(8,128)(2,1)} %constant.2.clone.table_ref) | copy-start | bytes 1179652
  1.9 17.4 %copy-start.4 = (f32[1,1,8,3,256]{4,2,3,1,0:T(8,128)S(1)}, f32[1,1,8,3,256]{4,2,3,1,0:T(8,128)}, u32[]{:S(2)}) copy-start(f32[1,1,8,3,256]{4,2,3,1,0:T(8,128)} %param.16) | copy-start | bytes 73732
  25.5 13.9 %copy-start.2 = (f32[7,8192]{1,0:T(8,128)S(1)}, f32[7,8192]{1,0:T(8,128)}, u32[]{:S(2)}) copy-start(f32[7,8192]{1,0:T(8,128)} %one_ref.1) | copy-start | bytes 688132
  25.5 13.9 %copy-start.3 = (f32[7,8192]{1,0:T(8,128)S(1)}, f32[7,8192]{1,0:T(8,128)}, u32[]{:S(2)}) copy-start(f32[7,8192]{1,0:T(8,128)} %two_ref.1) | copy-start | bytes 688132
  37.7 1.8 %copy-start = (f32[7,8192]{1,0:T(8,128)S(1)}, f32[7,8192]{1,0:T(8,128)}, u32[]{:S(2)}) copy-start(f32[7,8192]{1,0:T(8,128)} %params_ref.1) | copy-start | bytes 688132
  37.9 1.6 %collective-permute-start = (f32[448,128]{1,0:T(8,128)S(1)}, f32[448,128]{1,0:T(8,128)S(1)}, u32[]{:S(2)}, u32[]{:S(2)}) collective-permute-start(f32[448,128]{1,0:T(8,128)S(1)} %scatter.1.own_ref), channel_id=1, source_target_pairs={{0,1},{1,0},{2,3},{3,2},{4,5},{5,4},{6,7},{7,6},{8,9},{9,8},{10,11... | collective-permute-start | bytes 688136 | tf_op jit(solution)/shard_map/ppermute | solution.py:498
